TPU v7x, 512 devices: a whole 4x8x8 slice. The times are simulated.
512 devices in a mesh: ma: 64 (over z, x, core), ell: 8 (over y).
Axes of the slice: x: 4, y: 8, z: 8, core: 2. Of those that a mesh axis runs over, the one named last changes fastest.
Arguments:
- legendre: bfloat16 [3, 2048, 32, 4096], P(None, 'ma', None, 'ell'), may hold values from -6 to 6
- harmonics: bfloat16 [2048, 3, 2, 4, 4096], P('ma', None, None, None, 'ell'), may hold values from -0.0014648438 to 0.0014648438
- slot_orders: int32 [2048], replicated, may hold values from 0 to 2047, each once
- cycle_index: int32 [32], replicated, may hold values from 2048 to 4095
Outputs:
- maps: float32 [64, 3, 4, 8192], P('ma', None, None, 'ell')
Inputs may be any that keep to these rules, and one draw needn't show every extreme that they name: `slot_orders`: every number from 0 to 2047 appears once.
All inputs are finite; a program needn't handle non-finite values.
Results may differ from a plain program's by a relative error of at most 0.0003.
Values sent between devices are 32-bit elements; how exact they have to be, the bound alone decides.
No kernel may reach another device: no remote copies, remote signals or barrier semaphores. Data moves between devices by JAX's collectives and lax.ppermute only.
A program may use at most 64 MiB of HBM per device.

v0:
```python
import math

import jax
import jax.numpy as jnp
from jax import lax
from jax.sharding import PartitionSpec as P


def cut_along(shard, dim, peers):
    dims = shard.shape
    parts = shard.reshape(*dims[:dim], peers, dims[dim] // peers, *dims[dim + 1 :])
    return jnp.moveaxis(parts, dim, 0)


def sum_at_owner(shard, axis, dim):
    parts = cut_along(shard, dim, lax.axis_size(axis))
    arrived = lax.all_to_all(parts, axis, split_axis=0, concat_axis=0, tiled=True)
    return arrived.sum(axis=0)


def from_everyone(shard, axis):
    copies = jnp.broadcast_to(shard, (lax.axis_size(axis), *shard.shape))
    return lax.all_to_all(copies, axis, split_axis=0, concat_axis=0, tiled=True)


def joined_along(parts, dim):
    parts = jnp.moveaxis(parts, 0, dim)
    dims = parts.shape
    return parts.reshape(*dims[:dim], dims[dim] * dims[dim + 1], *dims[dim + 2 :])


def gathered_copies(shard, axis, dim):
    parts = from_everyone(shard, axis)
    return joined_along(parts, dim)


def column_weights(lower_order, first_column, columns_count, full_width):
    columns = first_column + jnp.arange(columns_count, dtype=jnp.int32)
    boundary = (full_width - 1 - lower_order)[:, None]
    lower_part = (columns[None, :] < boundary).astype(jnp.float32)
    upper_part = ((columns[None, :] >= boundary) & (columns[None, :] < full_width - 1)).astype(
        jnp.float32
    )
    lower_sign = (1 - 2 * (columns[None, :] % 2)).astype(jnp.float32)
    upper_sign = (1 - 2 * ((columns[None, :] + 1 + lower_order[:, None]) % 2)).astype(jnp.float32)
    return jnp.stack(
        [lower_part, lower_part * lower_sign, upper_part, upper_part * upper_sign], axis=1
    )


def spin_fields(plain, plus, minus):
    hemisphere = jnp.array([1.0, -1.0], jnp.float32).reshape(1, 1, 1, 2, 1, 1, 1)
    minus = minus * hemisphere
    temp_real = plain[:, :, :, :, 0]
    temp_imag = plain[:, :, :, :, 1]
    eplus_real = plus[:, :, :, :, 0, 0]
    eplus_imag = plus[:, :, :, :, 0, 1]
    bplus_real = plus[:, :, :, :, 1, 0]
    bplus_imag = plus[:, :, :, :, 1, 1]
    eminus_real = minus[:, :, :, :, 0, 0]
    eminus_imag = minus[:, :, :, :, 0, 1]
    bminus_real = minus[:, :, :, :, 1, 0]
    bminus_imag = minus[:, :, :, :, 1, 1]
    stokes_q_real = -(eplus_real - bminus_imag)
    stokes_q_imag = -(eplus_imag + bminus_real)
    stokes_u_real = -(bplus_real + eminus_imag)
    stokes_u_imag = -(bplus_imag - eminus_real)
    return jnp.stack(
        [
            jnp.stack([temp_real, temp_imag]),
            jnp.stack([stokes_q_real, stokes_q_imag]),
            jnp.stack([stokes_u_real, stokes_u_imag]),
        ]
    )


def place_orders(cycle_orders, lower_all):
    highest = lax.Precision.HIGHEST
    half = lower_all.shape[0]
    width = min(512, half)
    pieces = []
    for start in range(0, half, width):
        targets = start + jnp.arange(width, dtype=jnp.int32)
        onehot = (lower_all[:, None] == targets[None, :]).astype(jnp.float32)
        pieces.append(jnp.einsum("abcdes,sm->abcdem", cycle_orders, onehot, precision=highest))
    placed = jnp.concatenate(pieces, axis=-1)
    return jnp.concatenate([placed[..., 0, :], jnp.flip(placed[..., 1, :], axis=-1)], axis=-1)


def cycle_synthesis(coeff, shift, first_group, group_count):
    highest = lax.Precision.HIGHEST
    cycles_count = coeff.shape[0]
    components = coeff.shape[3]
    orders_count = coeff.shape[-1]
    pixels = 2 * orders_count
    outer = pixels // 128
    groups = orders_count // 128
    orders = jnp.arange(orders_count, dtype=jnp.int32)
    phase = (orders[None, :] * shift[:, None] % (2 * pixels)).astype(jnp.float32) * (
        math.pi / pixels
    )
    factor = jnp.where(orders == 0, 1.0, 2.0).astype(jnp.float32)
    cosine = (jnp.cos(phase) * factor)[:, None, None, :]
    sine = (jnp.sin(phase) * factor)[:, None, None, :]
    real_part = coeff[:, :, 0]
    imag_part = coeff[:, :, 1]
    shifted_real = (real_part * cosine - imag_part * sine).reshape(
        cycles_count, 3, components, groups, 128
    )
    shifted_imag = (real_part * sine + imag_part * cosine).reshape(
        cycles_count, 3, components, groups, 128
    )
    group_ids = jnp.arange(groups, dtype=jnp.int32)
    outer_ids = jnp.arange(outer, dtype=jnp.int32)
    inner_ids = jnp.arange(128, dtype=jnp.int32)
    angle_one = (group_ids[:, None] * outer_ids[None, :] % outer).astype(jnp.float32) * (
        2.0 * math.pi / outer
    )
    cos_one = jnp.cos(angle_one)
    sin_one = jnp.sin(angle_one)
    first_real = jnp.einsum(
        "xyzab,ak->xyzkb", shifted_real, cos_one, precision=highest
    ) - jnp.einsum("xyzab,ak->xyzkb", shifted_imag, sin_one, precision=highest)
    first_imag = jnp.einsum(
        "xyzab,ak->xyzkb", shifted_real, sin_one, precision=highest
    ) + jnp.einsum("xyzab,ak->xyzkb", shifted_imag, cos_one, precision=highest)
    angle_two = (outer_ids[:, None] * inner_ids[None, :] % pixels).astype(jnp.float32) * (
        2.0 * math.pi / pixels
    )
    cos_two = jnp.cos(angle_two)
    sin_two = jnp.sin(angle_two)
    twist_real = first_real * cos_two - first_imag * sin_two
    twist_imag = first_real * sin_two + first_imag * cos_two
    local_ids = first_group + jnp.arange(group_count, dtype=jnp.int32)
    angle_three = (inner_ids[:, None] * local_ids[None, :] % 128).astype(jnp.float32) * (
        2.0 * math.pi / 128
    )
    cos_three = jnp.cos(angle_three)
    sin_three = jnp.sin(angle_three)
    result = jnp.einsum("xyzkb,bq->xyzqk", twist_real, cos_three, precision=highest) - jnp.einsum(
        "xyzkb,bq->xyzqk", twist_imag, sin_three, precision=highest
    )
    return result.reshape(cycles_count, 3, components, group_count * outer)


def body(legendre, harmonics, slot_orders, cycle_index):
    ma_count = lax.axis_size("ma")
    ell_count = lax.axis_size("ell")
    slots_here = harmonics.shape[0]
    columns_here = harmonics.shape[-1]
    components = harmonics.shape[3]
    full_width = 2 * slot_orders.shape[0]
    pairs = cycle_index.shape[0]
    lower_here = lax.dynamic_slice_in_dim(
        slot_orders, lax.axis_index("ma") * slots_here, slots_here
    )
    weights = column_weights(
        lower_here, lax.axis_index("ell") * columns_here, columns_here, full_width
    ).astype(jnp.bfloat16)
    packed = harmonics[:, None] * weights[:, :, None, None, None, :]
    plain = jnp.einsum(
        "srj,sqpcj->srqpc", legendre[0], packed[:, :, 0], preferred_element_type=jnp.float32
    )
    plus = jnp.einsum(
        "srj,sqkpcj->srqkpc", legendre[1], packed[:, :, 1:3], preferred_element_type=jnp.float32
    )
    minus = jnp.einsum(
        "srj,sqkpcj->srqkpc", legendre[2], packed[:, :, 1:3], preferred_element_type=jnp.float32
    )
    plain = plain.reshape(slots_here, pairs, 2, 2, 2, components)
    plus = plus.reshape(slots_here, pairs, 2, 2, 2, 2, components)
    minus = minus.reshape(slots_here, pairs, 2, 2, 2, 2, components)
    fields = spin_fields(plain, plus, minus)
    cycle_sums = fields.transpose(5, 3, 0, 1, 6, 4, 2).reshape(
        2 * pairs, 3, 2, components, 2, slots_here
    )
    shares = sum_at_owner(cycle_sums, "ell", 5)
    moved = lax.all_to_all(shares, "ma", split_axis=0, concat_axis=5, tiled=True)
    cycle_orders = gathered_copies(moved, "ell", 5)
    portion = slots_here // ell_count
    positions = jnp.arange(slot_orders.shape[0], dtype=jnp.int32)
    block_index = positions // (ma_count * portion)
    source_index = positions % (ma_count * portion) // portion
    offset_index = positions % portion
    slot_ids = source_index * slots_here + block_index * portion + offset_index
    lower_all = slot_orders[slot_ids]
    coeff = place_orders(cycle_orders, lower_all)
    cycles_here = cycle_orders.shape[0]
    cycle_ids = lax.axis_index("ma") * cycles_here + jnp.arange(cycles_here, dtype=jnp.int32)
    shift = cycle_index[cycle_ids % pairs] % 2
    per_device = 128 // ell_count
    return cycle_synthesis(coeff, shift, lax.axis_index("ell") * per_device, per_device)


def solution(mesh):
    return jax.shard_map(
        body,
        mesh=mesh,
        in_specs=(P(None, "ma", None, "ell"), P("ma", None, None, None, "ell"), P(), P()),
        out_specs=P("ma", None, None, "ell"),
        check_vma=False,
    )
```

profile of v0, /device:TPU:1, one launch (start us, length us, event | category | flops | bytes accessed | tf_op | source)
XLA Modules:
  0.0 106.2 jit_solution(7492669706483582841)
XLA Ops:
  0.0 0.9 broadcast_subtract_fusion
  1.0 0.2 fusion.76
  1.2 0.1 fusion.74
  1.3 0.4 fusion.73
  1.7 0.3 pad_maximum_fusion.2
  2.0 3.3 %broadcast_multiply_fusion = bf16[32,4,3,2,4,512]{5,4,3,1,0,2:T(4,128)(2,1)S(1)} fusion(bf16[32,4,512]{2,1,0:T(4,128)(2,1)S(1)} %pad_maximum_fusion.2, bf16[32,3,2,4,512]{4,3,2,1,0:T(4,128)(2,1)} %param.6), kind=kLoop, calls=%fused_computation.25 | loop fusion | flops 6291456 | bytes 4063232 | tf_op jit(solution)/shard_map/mul | solution.py:160
  5.4 0.0 copy-done.2
  5.4 0.6 fusion.38
  6.0 1.0 fusion.21
  6.9 1.0 fusion.19
  7.9 0.0 copy-start.1
  7.9 0.1 fusion.153
  8.0 0.1 copy.80
  8.2 0.1 copy.81
  8.3 0.2 fusion.152
  8.5 0.3 maximum_bitcast_fusion.1
  8.8 0.7 copy_multiply_fusion
  9.5 0.8 fusion.61
  10.3 0.3 maximum_bitcast_fusion.2
  10.6 0.3 maximum_bitcast_fusion.3
  10.9 0.8 maximum_bitcast_fusion
  11.7 1.1 %reshape_reshape.3 = f32[64,3,2,4,2,8,4]{0,6,5,4,3,2,1:T(4,128)S(1)} reshape(f32[2,32,3,2,4,2,32]{1,0,6,5,4,3,2:T(2,128)S(1)} %maximum_bitcast_fusion) | data formatting | bytes 786432 | tf_op jit(solution)/shard_map/reshape;reshape | solution.py:11
  12.8 0.2 copy_bitcast_fusion.2
  13.0 0.7 reshape.851
  13.8 19.9 %all_to_all.28 = f32[8,1,12288]{2,1,0:T(1,128)S(1)} all-to-all(f32[8,1,12288]{2,1,0:T(1,128)S(1)} %reshape.851), channel_id=1, replica_groups=mesh['ma'=64,'ell'=8] {'ell'}, dimensions={0} | all-to-all | bytes 786432 | tf_op jit(solution)/shard_map/all_to_all | solution.py:17
  33.7 0.5 broadcast.810
  34.2 1.5 %reduce = f32[8,12288]{1,0:T(8,128)S(1)} reduce(f32[8,1,12288]{2,1,0:T(1,128)S(1)} %all_to_all.28, f32[]{:T(128)} %broadcast.810), dimensions={1}, to_apply=%all_to_all.19.reduce_sub_computation | reduce | bytes 786436 | tf_op jit(solution)/shard_map/all_to_all | solution.py:17
  35.7 0.5 reshape.852
  36.2 0.2 bitcast_reduce_fusion
  36.4 1.4 %copy.40 = f32[64,3,2,4,2,4]{5,4,3,2,1,0:T(2,128)S(1)} copy(f32[64,3,2,4,2,4]{0,5,4,3,2,1:T(4,128)S(1)} %bitcast_reduce_fusion) | data formatting | bytes 98304 | tf_op jit(solution)/shard_map/reduce_sum | solution.py:18
  37.8 3.0 %reshape.853 = f32[64,1,192]{2,1,0:T(1,128)} reshape(f32[64,3,2,4,2,4]{5,4,3,2,1,0:T(2,128)S(1)} %copy.40) | data formatting | bytes 98304
  40.8 16.5 %all-to-all-start.1 = ((f32[64,1,192]{2,1,0:T(1,128)}), f32[64,1,192]{2,1,0:T(1,128)S(1)}, u32[]{:S(2)}, u32[]{:S(2)}) async-start(f32[64,1,192]{2,1,0:T(1,128)} %reshape.853), calls=%async_computation.1 | async-start | bytes 131072 | tf_op jit(solution)/shard_map/all_to_all | solution.py:178
  57.4 10.0 %all-to-all-done.1 = f32[64,1,192]{2,1,0:T(1,128)S(1)} async-done(((f32[64,1,192]{2,1,0:T(1,128)}), f32[64,1,192]{2,1,0:T(1,128)S(1)}, u32[]{:S(2)}, u32[]{:S(2)}) %all-to-all-start.1) | async-done | bytes 49184 | tf_op jit(solution)/shard_map/all_to_all | solution.py:178
  67.4 0.7 reduce.1
  68.1 2.3 %reshape.854 = f32[64,3,2,4,2,4]{5,4,3,2,1,0:T(2,128)S(1)} reshape(f32[64,192]{1,0:T(8,128)S(1)} %reduce.1) | data formatting | bytes 98304
  70.5 0.0 copy-start.3
  70.5 0.0 copy-start
  70.5 0.5 copy.56
  71.0 1.1 %reshape.850 = f32[3,2,4,2,256]{4,2,3,1,0:T(4,128)S(1)} reshape(f32[1,3,2,4,2,64,4]{6,5,3,4,2,1,0:T(8,128)S(1)} %copy.56) | data formatting | bytes 98304 | tf_op jit(solution)/shard_map/all_to_all | solution.py:178
  72.1 0.8 broadcast_in_dim.10
  73.0 3.7 %all-to-all-start.2 = ((f32[8,1,3,2,4,2,256]{6,4,5,3,2,1,0:T(4,128)}), f32[8,1,3,2,4,2,256]{6,4,5,3,2,1,0:T(4,128)S(1)}, u32[]{:S(2)}, u32[]{:S(2)}) async-start(f32[8,1,3,2,4,2,256]{6,4,5,3,2,1,0:T(4,128)} %broadcast_in_dim.10), calls=%async_computation.2 | async-start | bytes 786432 | tf_op jit(solution)/shard_map/all_to_all | solution.py:23
  76.7 0.7 dynamic-slice.2
  79.3 11.8 %gather_fusion = s32[2048]{0:T(1024)S(1)} fusion(s32[2048]{0:T(1024)S(1)} %copy-done, s32[2048]{0:T(1024)S(1)} %broadcast_clamp_fusion), kind=kCustom, calls=%fused_computation | custom fusion | bytes 24576 | tf_op jit(solution)/shard_map/gather | solution.py:186
  91.1 0.1 select_multiply_fusion
  91.2 0.1 fusion.95
  91.3 0.0 all-to-all-done.2
  91.4 0.2 copy.43
  91.6 0.2 reshape.806
  91.8 1.8 %fusion.34 = f32[1,3,2,4,2,512]{5,3,4,2,1,0:T(4,128)S(1)} fusion(f32[3,2,4,2,2048]{4,2,3,1,0:T(4,128)S(1)} %reshape.806, s32[2048]{0:T(1024)S(1)} %gather_fusion), kind=kOutput, calls=%fused_computation.33 | convolution fusion | flops 605028352 | bytes 499712 | tf_op jit(solution)/shard_map/abcdes,sm->abcdem/dot_general | solution.py:85
  93.6 1.7 %fusion.25 = f32[1,3,2,4,2,512]{5,3,4,2,1,0:T(4,128)S(1)} fusion(f32[3,2,4,2,2048]{4,2,3,1,0:T(4,128)S(1)} %reshape.806, s32[512]{0:T(512)S(1)} %iota_add_fusion.2, s32[2048]{0:T(1024)S(1)} %gather_fusion), kind=kOutput, calls=%fused_computation.30 | convolution fusion | flops 605028352 | bytes 501760 | tf_op jit(solution)/shard_map/abcdes,sm->abcdem/dot_general | solution.py:85
  95.3 1.7 %fusion.28 = f32[1,3,2,4,2,512]{5,3,4,2,1,0:T(4,128)S(1)} fusion(f32[3,2,4,2,2048]{4,2,3,1,0:T(4,128)S(1)} %reshape.806, s32[512]{0:T(512)S(1)} %iota_add_fusion.1, s32[2048]{0:T(1024)S(1)} %gather_fusion), kind=kOutput, calls=%fused_computation.31 | convolution fusion | flops 605028352 | bytes 501760 | tf_op jit(solution)/shard_map/abcdes,sm->abcdem/dot_general | solution.py:85
  97.0 1.7 %fusion.31 = f32[1,3,2,4,2,512]{5,3,4,2,1,0:T(4,128)S(1)} fusion(f32[3,2,4,2,2048]{4,2,3,1,0:T(4,128)S(1)} %reshape.806, s32[512]{0:T(512)S(1)} %iota_add_fusion, s32[2048]{0:T(1024)S(1)} %gather_fusion), kind=kOutput, calls=%fused_computation.32 | convolution fusion | flops 605028352 | bytes 501760 | tf_op jit(solution)/shard_map/abcdes,sm->abcdem/dot_general | solution.py:85
  98.8 0.1 pad_maximum_fusion
  98.9 1.6 %rev.4 = f32[1,3,2,4,2048]{4,3,2,1,0:T(4,128)S(1)} reverse(f32[1,3,2,4,2048]{4,3,2,1,0:T(4,128)S(1)} %get-tuple-element.31), dimensions={4} | reverse | bytes 393216 | tf_op jit(solution)/shard_map/jit(_flip)/rev | solution.py:87
  100.5 0.1 fusion.62
  100.6 0.1 squeeze.38
  100.7 0.1 squeeze.39
  100.9 0.6 fusion.78
  101.5 0.6 fusion.77
  102.1 0.6 fusion.24
  102.7 0.6 fusion.23
  103.3 1.1 %fusion.46 = f32[16,3,4,64]{3,0,2,1:T(8,128)S(1)} fusion(f32[64,1,3,4,128]{4,0,3,2,1:T(8,128)S(1)} %fusion.23, f32[64,1,3,4,128]{4,0,3,2,1:T(8,128)S(1)} %fusion.24, f32[64,128]{1,0:T(8,128)S(1)} %get-tuple-element.38, f32[64,128]{1,0:T(8,128)S(1)} %get-tuple-element.39, s32[16]{0:T(128)S(1)} %iota_add_fusion.4), kind=kOutput, calls=%fused_computation.52 | convolution fusion | flops 19197952 | bytes 901184 | tf_op jit(solution)/shard_map/xyzkb,bq->xyzqk/dot_general | solution.py:140
  104.4 1.1 %fusion.37 = f32[1,3,4,16,64]{4,3,2,1,0:T(8,128)S(1)} fusion(f32[16,3,4,64]{3,0,2,1:T(8,128)S(1)} %fusion.46, f32[64,1,3,4,128]{4,0,3,2,1:T(8,128)S(1)} %fusion.23, f32[64,1,3,4,128]{4,0,3,2,1:T(8,128)S(1)} %fusion.24, f32[64,128]{1,0:T(8,128)S(1)} %get-tuple-element.38, f32[64,128]{1,0:T(8,128)S(1)} %get-tuple-element.39, s32[16]{0:T(128)S(1)} %iota_add_fusion.4), kind=kOutput, calls=%fused_computation.35 | convolution fusion | flops 19210240 | bytes 950336 | tf_op jit(solution)/shard_map/xyzkb,bq->xyzqk/dot_general | solution.py:140
  105.5 0.7 reshape.809
  (14 shorter events, 0.1 us)
Async XLA Ops:
  0.0 5.4 %copy-start.2 = (bf16[3,32,32,512]{3,2,1,0:T(8,128)(2,1)S(1)}, bf16[3,32,32,512]{3,2,1,0:T(8,128)(2,1)}, u32[]{:S(2)}) copy-start(bf16[3,32,32,512]{3,2,1,0:T(8,128)(2,1)} %param.5) | copy-start | bytes 9437188
  7.9 0.9 copy-start.1
  40.8 26.6 %all-to-all-start.1 = ((f32[64,1,192]{2,1,0:T(1,128)}), f32[64,1,192]{2,1,0:T(1,128)S(1)}, u32[]{:S(2)}, u32[]{:S(2)}) async-start(f32[64,1,192]{2,1,0:T(1,128)} %reshape.853), calls=%async_computation.1 | async-start | bytes 131072 | tf_op jit(solution)/shard_map/all_to_all | solution.py:178
  70.5 6.2 %copy-start.3 = (s32[32]{0:T(128)S(1)}, s32[32]{0:T(128)}, u32[]{:S(2)}) copy-start(s32[32]{0:T(128)} %param.8) | copy-start | bytes 388
  70.5 8.8 %copy-start = (s32[2048]{0:T(1024)S(1)}, s32[2048]{0:T(1024)}, u32[]{:S(2)}) copy-start(s32[2048]{0:T(1024)} %param.7) | copy-start | bytes 24580
  73.0 18.4 %all-to-all-start.2 = ((f32[8,1,3,2,4,2,256]{6,4,5,3,2,1,0:T(4,128)}), f32[8,1,3,2,4,2,256]{6,4,5,3,2,1,0:T(4,128)S(1)}, u32[]{:S(2)}, u32[]{:S(2)}) async-start(f32[8,1,3,2,4,2,256]{6,4,5,3,2,1,0:T(4,128)} %broadcast_in_dim.10), calls=%async_computation.2 | async-start | bytes 786432 | tf_op jit(solution)/shard_map/all_to_all | solution.py:23
where the time goes:
time: 107 us; the launch traced here: 106 us
  local copies, waits for them, and re-layouts  28.4 us (27%)
  starting transfers between devices  20.2 us (19%)
  blocking collectives  19.9 us (19%)
  matrix products  14 us (13%)
  other arithmetic  11.3 us (11%)
  waiting for transfers between devices  10 us (9%)
  between operations  2.43 us (2%)
    all_to_all x1, blocking collectives, sum_at_owner(): lax.all_to_all(parts, axis, split_axis=0, concat_axis=0, tiled=True)  19.9 us
    all_to_all x1, starting transfers between devices, body(): lax.all_to_all(shares, 'ma', split_axis=0, concat_axis=5, tiled=True)  16.5 us
    gather x1, local copies, waits for them, and re-layouts, body(): lower_all = slot_orders[slot_ids]  11.8 us
    all_to_all x1, waiting for transfers between devices, body(): lax.all_to_all(shares, 'ma', split_axis=0, concat_axis=5, tiled=True)  10 us
    unnamed x15, local copies, waits for them, and re-layouts  7.1 us
    dot_general x4, matrix products, place_orders(): jnp.einsum('abcdes,sm->abcdem', cycle_orders, onehot, precision=highest)  6.93 us
    all_to_all x1, starting transfers between devices, from_everyone(): return lax.all_to_all(copies, axis, split_axis=0, concat_axis=0, tiled=True)  3.67 us
    mul x1, other arithmetic, body(): packed = harmonics[:, None] * weights[:, :, None, None, None, :]  3.35 us
  transfers between devices with their start and end apart: 2, of which 1 were waited for; matrix products, arithmetic and copies ran while one was open for 12% of the time, Pallas kernels for 0%

commit v1 on v0

v1 whole, which is shorter than its diff:
```python
import math

import jax
import jax.numpy as jnp
from jax import lax
from jax.experimental import pallas as pl
from jax.experimental.pallas import tpu as pltpu
from jax.sharding import PartitionSpec as P

F32 = jnp.float32
BF16 = jnp.bfloat16
NT = (((1,), (1,)), ((), ()))


def legendre_kernel(orders_ref, leg_ref, harm_ref, out_ref, pack_ref, acc_ref):
    group = pl.program_id(0)
    groups = pl.num_programs(0)
    pairs = leg_ref.shape[2]
    width = leg_ref.shape[3]
    full = orders_ref[0]
    column = orders_ref[1] + lax.broadcasted_iota(jnp.int32, (1, width), 1)
    column_sign = (1 - 2 * (column % 2)).astype(F32)
    half = lax.broadcasted_iota(jnp.int32, (8, width), 0) < 4
    for slot in range(8):
        lower = orders_ref[2 + group * 8 + slot]
        boundary = full - 1 - lower
        lower_part = jnp.where(column < boundary, 1.0, 0.0).astype(F32)
        upper_part = jnp.where((column >= boundary) & (column < full - 1), 1.0, 0.0).astype(F32)
        upper_sign = column_sign * (2 * (lower % 2) - 1).astype(F32)
        temp = harm_ref[slot, 0].astype(F32)
        emode = harm_ref[slot, 1].astype(F32)
        bmode = harm_ref[slot, 2].astype(F32)
        eturn = pltpu.roll(emode, 4, 0)
        eturn = jnp.where(half, eturn, -eturn)
        bturn = pltpu.roll(bmode, 4, 0)
        bturn = jnp.where(half, bturn, -bturn)
        for side in range(2):
            if side == 0:
                weights = (lower_part, upper_part)
                turned = weights
            else:
                weights = (lower_part * column_sign, upper_part * upper_sign)
                turned = (-weights[0], -weights[1])

            def rows(values, scales):
                return jnp.concatenate([values * scales[0], values * scales[1]], axis=0).astype(BF16)

            minus = (-weights[0], -weights[1])
            straight = (-turned[0], -turned[1])
            base = side * 32
            pack_ref[slot, base : base + 16, 0:width] = rows(emode, minus)
            pack_ref[slot, base : base + 16, width : 2 * width] = rows(bturn, turned)
            pack_ref[slot, base + 16 : base + 32, 0:width] = rows(bmode, minus)
            pack_ref[slot, base + 16 : base + 32, width : 2 * width] = rows(eturn, straight)
            pack_ref[slot, 64 + side * 16 : 80 + side * 16, 0:width] = rows(temp, weights)
        both = lax.dot_general(
            leg_ref[1, slot], pack_ref[slot, 0:64, 0:width], NT, preferred_element_type=F32
        ) + lax.dot_general(
            leg_ref[2, slot], pack_ref[slot, 0:64, width : 2 * width], NT, preferred_element_type=F32
        )
        plain = lax.dot_general(
            leg_ref[0, slot], pack_ref[slot, 64:96, 0:width], NT, preferred_element_type=F32
        )
        lanes = slice(16 * slot, 16 * slot + 16)
        for side in range(2):
            acc_ref[side * 3, :, lanes] = plain[:, 16 * side : 16 * side + 16]
            acc_ref[side * 3 + 1, :, lanes] = both[:, 32 * side : 32 * side + 16]
            acc_ref[side * 3 + 2, :, lanes] = both[:, 32 * side + 16 : 32 * side + 32]
    for side in range(2):
        for field in range(3):
            start = side * pairs * 12 + field * 4 + group
            out_ref[pl.ds(start, pairs, stride=12), :] = acc_ref[side * 3 + field]


def legendre_sums(legendre, harmonics, orders):
    slots, pairs, width = legendre.shape[1:]
    return pl.pallas_call(
        legendre_kernel,
        grid_spec=pltpu.PrefetchScalarGridSpec(
            num_scalar_prefetch=1,
            grid=(slots // 8,),
            in_specs=[
                pl.BlockSpec((3, 8, pairs, width), lambda g, o: (0, g, 0, 0)),
                pl.BlockSpec((8, 3, 8, width), lambda g, o: (g, 0, 0, 0)),
            ],
            out_specs=pl.BlockSpec((2 * pairs * 12, 128), lambda g, o: (0, 0)),
            scratch_shapes=[
                pltpu.VMEM((8, 96, 2 * width), BF16),
                pltpu.VMEM((6, pairs, 128), F32),
            ],
        ),
        out_shape=jax.ShapeDtypeStruct((2 * pairs * 12, 128), F32),
        name="legendre_sums",
    )(orders, legendre, harmonics)


def cos_sin(phase):
    quarter = (phase + 2048) >> 12
    x = (phase - (quarter << 12)).astype(F32) * (math.pi / 8192)
    y = x * x
    sine = x + x * y * (-1.6666667e-1 + y * (8.3333310e-3 + y * (-1.9840874e-4 + y * 2.7525562e-6)))
    cosine = 1.0 + y * (-0.5 + y * (4.16666642e-2 + y * (-1.38887875e-3 + y * 2.4760495e-5)))
    swap = (quarter & 1) == 1
    cos_out = jnp.where(swap, sine, cosine)
    sin_out = jnp.where(swap, cosine, sine)
    cos_flip = ((quarter + 1) & 2) == 2
    sin_flip = (quarter & 2) == 2
    return jnp.where(cos_flip, -cos_out, cos_out), jnp.where(sin_flip, -sin_out, sin_out)


def high_low(value):
    high = value.astype(BF16)
    return high, (value - high.astype(F32)).astype(BF16)


def tables_kernel(shift_ref, lower_ref, high_ref, low_ref, cos_ref, sin_ref):
    slots = high_ref.shape[2] // 2
    tiles = slots // 128
    row = lax.broadcasted_iota(jnp.int32, (16, 128), 0)

    @pl.loop(0, tiles)
    def _(tile):
        lower = lower_ref[pl.ds(tile, 1), :]
        odd = lower % 2
        lanes = pl.multiple_of(tile * 128, 128)
        for parity in range(2):
            order = jnp.where(odd == parity, lower, 4095 - lower)
            factor = jnp.where(order == 0, 1.0, 2.0).astype(F32)
            cosine, sine = cos_sin((order * (512 * row + shift_ref[0])) & 16383)
            cos_ref[parity, tile] = cosine * factor
            sin_ref[parity, tile] = sine * factor
            cos_v, sin_v = cos_sin((order * (2 * row)) & 16383)
            cos_u, sin_u = cos_sin((order * (32 * row)) & 16383)
            for u in range(16):
                cu = cos_u[u : u + 1, :]
                su = sin_u[u : u + 1, :]
                pixels = slice(16 * u, 16 * u + 16)
                high, low = high_low(cu * cos_v - su * sin_v)
                high_ref[parity, pixels, pl.ds(lanes, 128)] = high
                low_ref[parity, pixels, pl.ds(lanes, 128)] = low
                high, low = high_low(su * cos_v + cu * sin_v)
                high_ref[parity, pixels, pl.ds(slots + lanes, 128)] = high
                low_ref[parity, pixels, pl.ds(slots + lanes, 128)] = low


def tables(shift, lower, slots):
    vmem = pl.BlockSpec(memory_space=pltpu.VMEM)
    return pl.pallas_call(
        tables_kernel,
        in_specs=[pl.BlockSpec(memory_space=pltpu.SMEM), vmem],
        out_specs=[vmem] * 4,
        out_shape=[
            jax.ShapeDtypeStruct((2, 256, 2 * slots), BF16),
            jax.ShapeDtypeStruct((2, 256, 2 * slots), BF16),
            jax.ShapeDtypeStruct((2, slots // 128, 16, 128), F32),
            jax.ShapeDtypeStruct((2, slots // 128, 16, 128), F32),
        ],
        name="tables",
    )(shift, lower)


def synthesis_kernel(lower_ref, cos_ref, sin_ref, high_ref, low_ref, sums_ref, out_ref, x_ref, a_ref):
    slots = high_ref.shape[2] // 2
    tiles = slots // 128
    for field in range(3):
        for pair in range(2):
            first = sums_ref[pl.ds(field * 4 + pair * 2, 64, stride=12), :]
            second = sums_ref[pl.ds(field * 4 + pair * 2 + 1, 64, stride=12), :]
            turned = jnp.concatenate([first, second], axis=0).T
            x_ref[field, pair * 8 : pair * 8 + 8] = turned.reshape(8, 16, 128)

    @pl.loop(0, tiles)
    def _(tile):
        odd = (lower_ref[pl.ds(tile, 1), :] % 2) == 1
        lanes = pl.multiple_of(tile * 128, 128)
        for field in range(3):
            x = x_ref[field, tile]
            for parity in range(2):
                keep = odd if parity else jnp.logical_not(odd)
                chosen = jnp.where(keep, x[0:8], x[8:16])
                cosine = cos_ref[parity, tile]
                sine = sin_ref[parity, tile]
                for comp in range(4):
                    real = chosen[comp : comp + 1, :]
                    imag = chosen[4 + comp : 5 + comp, :]
                    rows = (field * 4 + comp) * 16
                    high, low = high_low(real * cosine - imag * sine)
                    a_ref[parity, rows : rows + 16, pl.ds(lanes, 128)] = high
                    a_ref[parity, 192 + rows : 208 + rows, pl.ds(lanes, 128)] = low
                    high, low = high_low(-(real * sine + imag * cosine))
                    a_ref[parity, rows : rows + 16, pl.ds(slots + lanes, 128)] = high
                    a_ref[parity, 192 + rows : 208 + rows, pl.ds(slots + lanes, 128)] = low

    parts = []
    for parity in range(2):
        wide = lax.dot_general(a_ref[parity], high_ref[parity], NT, preferred_element_type=F32)
        fine = lax.dot_general(a_ref[parity, 0:192, :], low_ref[parity], NT, preferred_element_type=F32)
        parts.append(wide[0:192] + (wide[192:384] + fine))
    near = parts[0] + parts[1]
    far = parts[0] - parts[1]
    for block in range(4):
        for row in range(12):
            place = slice(row * 4, row * 4 + 4)
            source = slice(row * 16 + block * 4, row * 16 + block * 4 + 4)
            out_ref[block, place, :] = near[source, :]
            out_ref[block + 4, place, :] = far[source, :]


def synthesis(lower, cosine, sine, high, low, sums):
    vmem = pl.BlockSpec(memory_space=pltpu.VMEM)
    slots = high.shape[2] // 2
    return pl.pallas_call(
        synthesis_kernel,
        in_specs=[vmem] * 6,
        out_specs=vmem,
        out_shape=jax.ShapeDtypeStruct((8, 48, 256), F32),
        scratch_shapes=[
            pltpu.VMEM((3, slots // 128, 16, 128), F32),
            pltpu.VMEM((2, 384, 2 * slots), BF16),
        ],
        name="synthesis",
    )(lower, cosine, sine, high, low, sums)


def total_kernel(parts_ref, out_ref, sum_ref):
    total = parts_ref[0]
    for source in range(1, 8):
        total = total + parts_ref[source]
    sum_ref[0] = total[:, 0:128]
    sum_ref[1] = total[:, 128:256]
    for field in range(3):
        for piece in range(4):
            for side in range(2):
                start = piece * 256 + side * 128
                out_ref[0, field, :, start : start + 128] = sum_ref[side, pl.ds(field * 16 + piece, 4, stride=4), :]


def total(parts):
    vmem = pl.BlockSpec(memory_space=pltpu.VMEM)
    return pl.pallas_call(
        total_kernel,
        in_specs=[vmem],
        out_specs=vmem,
        out_shape=jax.ShapeDtypeStruct((1, 3, 4, 1024), F32),
        scratch_shapes=[pltpu.VMEM((2, 48, 128), F32)],
        name="total",
    )(parts)


def body(legendre, harmonics, slot_orders, cycle_index):
    slots_here = harmonics.shape[0]
    columns_here = harmonics.shape[-1]
    slots = slot_orders.shape[0]
    pairs = cycle_index.shape[0]
    place = lax.axis_index("ma")
    lower_here = lax.dynamic_slice_in_dim(slot_orders, place * slots_here, slots_here)
    first_column = lax.axis_index("ell") * columns_here
    orders = jnp.concatenate([jnp.stack([jnp.int32(2 * slots), first_column.astype(jnp.int32)]), lower_here])
    sums = legendre_sums(legendre, harmonics.reshape(slots_here, 3, 8, columns_here), orders)
    moved = lax.all_to_all(sums.reshape(64, 3, 4, 128), "ma", split_axis=0, concat_axis=0, tiled=True)
    shift = lax.dynamic_slice_in_dim(cycle_index, place % pairs, 1) % 2
    lower = slot_orders.reshape(64, 2, 2, 8).transpose(1, 3, 2, 0).reshape(16, 128)
    high, low, cosine, sine = tables(shift, lower, slots)
    blocks = synthesis(lower, cosine, sine, high, low, moved.reshape(768, 128))
    arrived = lax.all_to_all(blocks, "ell", split_axis=0, concat_axis=0, tiled=True)
    return total(arrived)


def solution(mesh):
    return jax.shard_map(
        body,
        mesh=mesh,
        in_specs=(P(None, "ma", None, "ell"), P("ma", None, None, None, "ell"), P(), P()),
        out_specs=P("ma", None, None, "ell"),
        check_vma=False,
    )
```

time: 107 us -> 74.3 us (0.69)
  Pallas kernels: 0 us -> 27.2 us
  local copies, waits for them, and re-layouts: 28.4 us -> 5.44 us
  matrix products: 14 us -> 0 us
  other arithmetic: 11.3 us -> 0.58 us
  waiting for transfers between devices: 10 us -> 2.66 us
  starting transfers between devices: 20.2 us -> 14.8 us
  blocking collectives: 19.9 us -> 21.1 us
    pallas_call x0 -> x4, Pallas kernels: none -> 27.2 us  [the longest x1 11 us: synthesis(): pl.pallas_call(synthesis_kernel, in_specs=[vmem] * 6, out_specs=vmem, out...]
    dot_general x13 -> x0, matrix products: 14 us -> none  [the longest x4 6.93 us: place_orders(): jnp.einsum('abcdes,sm->abcdem', cycle_orders, onehot, precision=highest)]
    gather x2 -> x0, local copies, waits for them, and re-layouts: 12.4 us -> none  [the longest x1 11.8 us: body(): lower_all = slot_orders[slot_ids]]
    all_to_all x2 -> x1, waiting for transfers between devices: 10 us -> 2.66 us  [body(): lax.all_to_all(sums.reshape(64, 3, 4, 128), 'ma', split_axis=0, concat_ax...]
    unnamed x15 -> x6, local copies, waits for them, and re-layouts: 7.1 us -> 0.8 us
    all_to_all x2 -> x1, starting transfers between devices: 20.2 us -> 14.8 us  [body(): lax.all_to_all(sums.reshape(64, 3, 4, 128), 'ma', split_axis=0, concat_ax...]
    mul x3 -> x0, other arithmetic: 4.1 us -> none  [the longest x1 3.35 us: body(): packed = harmonics[:, None] * weights[:, :, None, None, None, :]]
    reshape x1 -> x3, local copies, waits for them, and re-layouts: 0.74 us -> 3.21 us  [the longest x1 2.28 us: body(): harmonics.reshape(slots_here, 3, 8, columns_here)]
  transfers between devices with their start and end apart: 2 -> 1, of which waited for: 1 -> 1; matrix products, arithmetic and copies ran while one was open for 12% -> 2% of each run, Pallas kernels for 0% -> 12%
where the time goes in v1:
time: 74.3 us; the launch traced here: 73.8 us
  Pallas kernels  27.2 us (37%)
  blocking collectives  21.1 us (28%)
  starting transfers between devices  14.8 us (20%)
  local copies, waits for them, and re-layouts  5.44 us (7%)
  waiting for transfers between devices  2.66 us (4%)
  between operations  2.01 us (3%)
    all_to_all x1, blocking collectives, body(): lax.all_to_all(blocks, 'ell', split_axis=0, concat_axis=0, tiled=True)  21.1 us
    all_to_all x1, starting transfers between devices, body(): lax.all_to_all(sums.reshape(64, 3, 4, 128), 'ma', split_axis=0, concat_ax...  14.8 us
    pallas_call x1, Pallas kernels, synthesis(): pl.pallas_call(synthesis_kernel, in_specs=[vmem] * 6, out_specs=vmem, out...  11 us
    pallas_call x1, Pallas kernels, tables(): pl.pallas_call(tables_kernel, in_specs=[pl.BlockSpec(memory_space=pltpu.S...  8.91 us
    pallas_call x1, Pallas kernels, legendre_sums(): pl.pallas_call(legendre_kernel, grid_spec=pltpu.PrefetchScalarGridSpec(nu...  5.69 us
    all_to_all x1, waiting for transfers between devices, body(): lax.all_to_all(sums.reshape(64, 3, 4, 128), 'ma', split_axis=0, concat_ax...  2.66 us
    reshape x1, local copies, waits for them, and re-layouts, body(): harmonics.reshape(slots_here, 3, 8, columns_here)  2.28 us
    pallas_call x1, Pallas kernels, total(): pl.pallas_call(total_kernel, in_specs=[vmem], out_specs=vmem, out_shape=j...  1.65 us
  transfers between devices with their start and end apart: 1, of which 1 were waited for; matrix products, arithmetic and copies ran while one was open for 2% of the time, Pallas kernels for 12%

profile of v1, /device:TPU:1, one launch (start us, length us, event | category | flops | bytes accessed | tf_op | source)
XLA Modules:
  0.0 73.8 jit_solution(16255910282307338510)
XLA Ops:
  0.0 0.0 copy-start.1
  0.0 0.0 copy-start.2
  0.0 2.3 %reshape.19.harm_ref = bf16[32,3,8,512]{3,2,1,0:T(8,128)(2,1)} reshape(bf16[32,3,2,4,512]{4,3,2,1,0:T(4,128)(2,1)} %param.5) | data formatting | bytes 1572864 | tf_op jit(solution)/shard_map/reshape | solution.py:259
  2.3 0.8 %dynamic_slice.7 = s32[32]{0:T(128)S(1)} dynamic-slice(s32[2048]{0:T(1024)} %param.6, s32[]{:T(128)S(6)} %select_n.22), dynamic_slice_sizes={32} | dynamic-slice | bytes 260 | tf_op jit(solution)/shard_map/dynamic_slice | solution.py:256
  3.0 0.6 pad_add_fusion.orders_ref
  3.6 5.7 %legendre_sums.1 = f32[768,128]{1,0:T(8,128)} custom-call(s32[34]{0:T(128)} %pad_add_fusion.orders_ref, bf16[3,32,32,512]{3,2,1,0:T(8,128)(2,1)} %leg_ref.1, bf16[32,3,8,512]{3,2,1,0:T(8,128)(2,1)} %reshape.19.harm_ref), custom_call_target="tpu_custom_call" | custom-call | tf_op jit(solution)/shard_map/legendre_sums/pallas_call | solution.py:77
  9.3 14.8 %all-to-all-start = ((f32[64,3,4,128]{3,2,1,0:T(4,128)}), f32[64,3,4,128]{3,2,1,0:T(4,128)S(1)}, u32[]{:S(2)}, u32[]{:S(2)}) async-start(f32[64,3,4,128]{3,2,1,0:T(4,128)} %bitcast.5), calls=%async_computation | async-start | bytes 786432 | tf_op jit(solution)/shard_map/all_to_all | solution.py:260
  24.2 0.0 copy-done.2
  24.2 0.6 dynamic_slice.6
  26.7 0.0 copy-done.1
  26.7 0.2 reshape.17
  27.0 0.1 copy.5
  27.0 0.7 reshape.18.lower_ref
  27.7 8.9 %tables.1 = (bf16[2,256,4096]{2,1,0:T(8,128)(2,1)}, bf16[2,256,4096]{2,1,0:T(8,128)(2,1)}, f32[2,16,16,128]{3,2,1,0:T(8,128)}, f32[2,16,16,128]{3,2,1,0:T(8,128)}) custom-call(s32[1]{0:T(128)S(6)} %select_n.21.shift_ref, s32[16,128]{1,0:T(8,128)} %reshape.18.lower_ref), custom_call_target="tpu_custom_call" | custom-call | tf_op jit(solution)/shard_map/tables/pallas_call | solution.py:148
  36.7 2.7 %all-to-all-done = f32[64,3,4,128]{3,2,1,0:T(4,128)S(1)} async-done(((f32[64,3,4,128]{3,2,1,0:T(4,128)}), f32[64,3,4,128]{3,2,1,0:T(4,128)S(1)}, u32[]{:S(2)}, u32[]{:S(2)}) %all-to-all-start) | async-done | bytes 393248 | tf_op jit(solution)/shard_map/all_to_all | solution.py:260
  39.3 0.0 copy-start
  39.3 0.8 %copy-done = f32[64,3,4,128]{3,2,1,0:T(4,128)} copy-done((f32[64,3,4,128]{3,2,1,0:T(4,128)}, f32[64,3,4,128]{3,2,1,0:T(4,128)S(1)}, u32[]{:S(2)}) %copy-start) | copy-done | bytes 393240
  40.1 11.0 %synthesis.1 = f32[8,48,256]{2,1,0:T(8,128)} custom-call(s32[16,128]{1,0:T(8,128)} %reshape.18.lower_ref, f32[2,16,16,128]{3,2,1,0:T(8,128)} %get-tuple-element.9.cos_ref, f32[2,16,16,128]{3,2,1,0:T(8,128)} %get-tuple-element.10.sin_ref, bf16[2,256,4096]{2,1,0:T(8,128)(2,1)} %get-tuple-element.11.high_ref, bf16[2,256,4096]{2,1,0:T(8,128)(2,1)} %get-tuple-element.12.low_ref, ...), custom_call_target="tpu_custom_call" | custom-call | tf_op jit(solution)/shard_map/synthesis/pallas_call | solution.py:212
  51.1 21.1 %all_to_all.10.parts_ref = f32[8,48,256]{2,1,0:T(8,128)} all-to-all(f32[8,48,256]{2,1,0:T(8,128)} %synthesis.1), channel_id=1, replica_groups=mesh['ma'=64,'ell'=8] {'ell'}, dimensions={0} | all-to-all | bytes 786432 | tf_op jit(solution)/shard_map/all_to_all | solution.py:265
  72.2 1.6 %total.1 = f32[1,3,4,1024]{3,2,1,0:T(4,128)} custom-call(f32[8,48,256]{2,1,0:T(8,128)} %all_to_all.10.parts_ref), custom_call_target="tpu_custom_call" | custom-call | tf_op jit(solution)/shard_map/total/pallas_call | solution.py:240
Async XLA Ops:
  0.0 26.7 %copy-start.1 = (s32[2048]{0:T(1024)S(1)}, s32[2048]{0:T(1024)}, u32[]{:S(2)}) copy-start(s32[2048]{0:T(1024)} %param.6) | copy-start | bytes 24580
  0.0 24.2 %copy-start.2 = (s32[32]{0:T(128)S(1)}, s32[32]{0:T(128)}, u32[]{:S(2)}) copy-start(s32[32]{0:T(128)} %param.7) | copy-start | bytes 388
  9.3 30.0 %all-to-all-start = ((f32[64,3,4,128]{3,2,1,0:T(4,128)}), f32[64,3,4,128]{3,2,1,0:T(4,128)S(1)}, u32[]{:S(2)}, u32[]{:S(2)}) async-start(f32[64,3,4,128]{3,2,1,0:T(4,128)} %bitcast.5), calls=%async_computation | async-start | bytes 786432 | tf_op jit(solution)/shard_map/all_to_all | solution.py:260
  39.3 0.8 %copy-start = (f32[64,3,4,128]{3,2,1,0:T(4,128)}, f32[64,3,4,128]{3,2,1,0:T(4,128)S(1)}, u32[]{:S(2)}) copy-start(f32[64,3,4,128]{3,2,1,0:T(4,128)S(1)} %all-to-all-done) | copy-start | bytes 1179652

commit v2 on v1

--- a/solution.py
+++ b/solution.py
@@ -17,19 +17,21 @@
     groups = pl.num_programs(0)
     pairs = leg_ref.shape[2]
     width = leg_ref.shape[3]
-    full = orders_ref[0]
-    column = orders_ref[1] + lax.broadcasted_iota(jnp.int32, (1, width), 1)
+    full = 2 * orders_ref.shape[0]
+    first_slot = lax.axis_index("ma") * (8 * groups) + group * 8
+    column = lax.axis_index("ell") * width + lax.broadcasted_iota(jnp.int32, (1, width), 1)
     column_sign = (1 - 2 * (column % 2)).astype(F32)
     half = lax.broadcasted_iota(jnp.int32, (8, width), 0) < 4
     for slot in range(8):
-        lower = orders_ref[2 + group * 8 + slot]
+        lower = orders_ref[first_slot + slot]
         boundary = full - 1 - lower
         lower_part = jnp.where(column < boundary, 1.0, 0.0).astype(F32)
         upper_part = jnp.where((column >= boundary) & (column < full - 1), 1.0, 0.0).astype(F32)
         upper_sign = column_sign * (2 * (lower % 2) - 1).astype(F32)
-        temp = harm_ref[slot, 0].astype(F32)
-        emode = harm_ref[slot, 1].astype(F32)
-        bmode = harm_ref[slot, 2].astype(F32)
+        temp, emode, bmode = (
+            jnp.concatenate([harm_ref[slot, kind, part].astype(F32) for part in range(2)], axis=0)
+            for kind in range(3)
+        )
         eturn = pltpu.roll(emode, 4, 0)
         eturn = jnp.where(half, eturn, -eturn)
         bturn = pltpu.roll(bmode, 4, 0)
@@ -81,7 +83,7 @@
             grid=(slots // 8,),
             in_specs=[
                 pl.BlockSpec((3, 8, pairs, width), lambda g, o: (0, g, 0, 0)),
-                pl.BlockSpec((8, 3, 8, width), lambda g, o: (g, 0, 0, 0)),
+                pl.BlockSpec((8, 3, 2, 4, width), lambda g, o: (g, 0, 0, 0, 0)),
             ],
             out_specs=pl.BlockSpec((2 * pairs * 12, 128), lambda g, o: (0, 0)),
             scratch_shapes=[
@@ -113,20 +115,29 @@
     return high, (value - high.astype(F32)).astype(BF16)
 
 
-def tables_kernel(shift_ref, lower_ref, high_ref, low_ref, cos_ref, sin_ref):
+def tables_kernel(cycle_ref, slots_ref, lower_ref, cos_ref, sin_ref, high_ref, low_ref, high_buf, low_buf, sem):
     slots = high_ref.shape[2] // 2
     tiles = slots // 128
+    shift = cycle_ref[lax.axis_index("ma") % cycle_ref.shape[0]] % 2
     row = lax.broadcasted_iota(jnp.int32, (16, 128), 0)
-
-    @pl.loop(0, tiles)
-    def _(tile):
+    turned = slots_ref[...].astype(F32).T
+    pieces = []
+    for middle in range(2):
+        for device in range(4):
+            start = device * 32 + middle * 8
+            pieces.append(
+                jnp.concatenate([turned[start : start + 8], turned[start + 16 : start + 24]], axis=0)
+            )
+    lower_ref[...] = jnp.concatenate(pieces, axis=1).astype(jnp.int32)
+
+    def one_tile(tile):
         lower = lower_ref[pl.ds(tile, 1), :]
         odd = lower % 2
         lanes = pl.multiple_of(tile * 128, 128)
         for parity in range(2):
             order = jnp.where(odd == parity, lower, 4095 - lower)
             factor = jnp.where(order == 0, 1.0, 2.0).astype(F32)
-            cosine, sine = cos_sin((order * (512 * row + shift_ref[0])) & 16383)
+            cosine, sine = cos_sin((order * (512 * row + shift)) & 16383)
             cos_ref[parity, tile] = cosine * factor
             sin_ref[parity, tile] = sine * factor
             cos_v, sin_v = cos_sin((order * (2 * row)) & 16383)
@@ -136,37 +147,71 @@
                 su = sin_u[u : u + 1, :]
                 pixels = slice(16 * u, 16 * u + 16)
                 high, low = high_low(cu * cos_v - su * sin_v)
-                high_ref[parity, pixels, pl.ds(lanes, 128)] = high
-                low_ref[parity, pixels, pl.ds(lanes, 128)] = low
+                high_buf[parity, pixels, pl.ds(lanes, 128)] = high
+                low_buf[parity, pixels, pl.ds(lanes, 128)] = low
                 high, low = high_low(su * cos_v + cu * sin_v)
-                high_ref[parity, pixels, pl.ds(slots + lanes, 128)] = high
-                low_ref[parity, pixels, pl.ds(slots + lanes, 128)] = low
-
-
-def tables(shift, lower, slots):
+                high_buf[parity, pixels, pl.ds(slots + lanes, 128)] = high
+                low_buf[parity, pixels, pl.ds(slots + lanes, 128)] = low
+
+    copies = []
+    span = 4
+    for block in range(tiles // span):
+        pl.loop(block * span, (block + 1) * span)(one_tile)
+        for parity in range(2):
+            for part in range(2):
+                for buf, ref in ((high_buf, high_ref), (low_buf, low_ref)):
+                    view = (parity, slice(None), pl.ds(part * slots + block * span * 128, span * 128))
+                    copy = pltpu.make_async_copy(buf.at[view], ref.at[view], sem.at[len(copies)])
+                    copy.start()
+                    copies.append(copy)
+    for copy in copies:
+        copy.wait()
+
+
+def tables(cycle_index, slot_orders):
+    slots = slot_orders.shape[0]
     vmem = pl.BlockSpec(memory_space=pltpu.VMEM)
+    hbm = pl.BlockSpec(memory_space=pltpu.HBM)
+    small = jax.ShapeDtypeStruct((2, slots // 128, 16, 128), F32)
+    large = jax.ShapeDtypeStruct((2, 256, 2 * slots), BF16)
     return pl.pallas_call(
         tables_kernel,
         in_specs=[pl.BlockSpec(memory_space=pltpu.SMEM), vmem],
-        out_specs=[vmem] * 4,
-        out_shape=[
-            jax.ShapeDtypeStruct((2, 256, 2 * slots), BF16),
-            jax.ShapeDtypeStruct((2, 256, 2 * slots), BF16),
-            jax.ShapeDtypeStruct((2, slots // 128, 16, 128), F32),
-            jax.ShapeDtypeStruct((2, slots // 128, 16, 128), F32),
+        out_specs=[vmem, vmem, vmem, hbm, hbm],
+        out_shape=[jax.ShapeDtypeStruct((slots // 128, 128), jnp.int32), small, small, large, large],
+        scratch_shapes=[
+            pltpu.VMEM((2, 256, 2 * slots), BF16),
+            pltpu.VMEM((2, 256, 2 * slots), BF16),
+            pltpu.SemaphoreType.DMA((slots // 64,)),
         ],
+        compiler_params=pltpu.CompilerParams(vmem_limit_bytes=60 << 20),
         name="tables",
-    )(shift, lower)
-
-
-def synthesis_kernel(lower_ref, cos_ref, sin_ref, high_ref, low_ref, sums_ref, out_ref, x_ref, a_ref):
+    )(cycle_index, slot_orders.reshape(slots // 128, 128))
+
+
+def synthesis_kernel(
+    lower_ref, cos_ref, sin_ref, high_ref, low_ref, sums_ref, out_ref, x_ref, a_ref, high_buf, low_buf, sem
+):
     slots = high_ref.shape[2] // 2
     tiles = slots // 128
+    copies = [
+        [
+            pltpu.make_async_copy(ref.at[parity], buf.at[parity], sem.at[2 * parity + i])
+            for i, (ref, buf) in enumerate(((high_ref, high_buf), (low_ref, low_buf)))
+        ]
+        for parity in range(2)
+    ]
+    for pair in copies:
+        for copy in pair:
+            copy.start()
     for field in range(3):
         for pair in range(2):
-            first = sums_ref[pl.ds(field * 4 + pair * 2, 64, stride=12), :]
-            second = sums_ref[pl.ds(field * 4 + pair * 2 + 1, 64, stride=12), :]
-            turned = jnp.concatenate([first, second], axis=0).T
+            pieces = []
+            for middle in range(2):
+                for device in range(4):
+                    start = device * 12 + field * 4 + pair * 2 + middle
+                    pieces.append(sums_ref[pl.ds(start, 16, stride=48), :])
+            turned = jnp.concatenate(pieces, axis=0).T
             x_ref[field, pair * 8 : pair * 8 + 8] = turned.reshape(8, 16, 128)
 
     @pl.loop(0, tiles)
@@ -193,8 +238,10 @@
 
     parts = []
     for parity in range(2):
-        wide = lax.dot_general(a_ref[parity], high_ref[parity], NT, preferred_element_type=F32)
-        fine = lax.dot_general(a_ref[parity, 0:192, :], low_ref[parity], NT, preferred_element_type=F32)
+        for copy in copies[parity]:
+            copy.wait()
+        wide = lax.dot_general(a_ref[parity], high_buf[parity], NT, preferred_element_type=F32)
+        fine = lax.dot_general(a_ref[parity, 0:192, :], low_buf[parity], NT, preferred_element_type=F32)
         parts.append(wide[0:192] + (wide[192:384] + fine))
     near = parts[0] + parts[1]
     far = parts[0] - parts[1]
@@ -208,16 +255,21 @@
 
 def synthesis(lower, cosine, sine, high, low, sums):
     vmem = pl.BlockSpec(memory_space=pltpu.VMEM)
+    hbm = pl.BlockSpec(memory_space=pltpu.HBM)
     slots = high.shape[2] // 2
     return pl.pallas_call(
         synthesis_kernel,
-        in_specs=[vmem] * 6,
+        in_specs=[vmem, vmem, vmem, hbm, hbm, vmem],
         out_specs=vmem,
         out_shape=jax.ShapeDtypeStruct((8, 48, 256), F32),
         scratch_shapes=[
             pltpu.VMEM((3, slots // 128, 16, 128), F32),
             pltpu.VMEM((2, 384, 2 * slots), BF16),
+            pltpu.VMEM((2, 256, 2 * slots), BF16),
+            pltpu.VMEM((2, 256, 2 * slots), BF16),
+            pltpu.SemaphoreType.DMA((4,)),
         ],
+        compiler_params=pltpu.CompilerParams(vmem_limit_bytes=60 << 20),
         name="synthesis",
     )(lower, cosine, sine, high, low, sums)
 
@@ -243,24 +295,15 @@
         out_specs=vmem,
         out_shape=jax.ShapeDtypeStruct((1, 3, 4, 1024), F32),
         scratch_shapes=[pltpu.VMEM((2, 48, 128), F32)],
+        compiler_params=pltpu.CompilerParams(vmem_limit_bytes=8 << 20),
         name="total",
     )(parts)
 
 
 def body(legendre, harmonics, slot_orders, cycle_index):
-    slots_here = harmonics.shape[0]
-    columns_here = harmonics.shape[-1]
-    slots = slot_orders.shape[0]
-    pairs = cycle_index.shape[0]
-    place = lax.axis_index("ma")
-    lower_here = lax.dynamic_slice_in_dim(slot_orders, place * slots_here, slots_here)
-    first_column = lax.axis_index("ell") * columns_here
-    orders = jnp.concatenate([jnp.stack([jnp.int32(2 * slots), first_column.astype(jnp.int32)]), lower_here])
-    sums = legendre_sums(legendre, harmonics.reshape(slots_here, 3, 8, columns_here), orders)
+    sums = legendre_sums(legendre, harmonics, slot_orders)
     moved = lax.all_to_all(sums.reshape(64, 3, 4, 128), "ma", split_axis=0, concat_axis=0, tiled=True)
-    shift = lax.dynamic_slice_in_dim(cycle_index, place % pairs, 1) % 2
-    lower = slot_orders.reshape(64, 2, 2, 8).transpose(1, 3, 2, 0).reshape(16, 128)
-    high, low, cosine, sine = tables(shift, lower, slots)
+    lower, cosine, sine, high, low = tables(cycle_index, slot_orders)
     blocks = synthesis(lower, cosine, sine, high, low, moved.reshape(768, 128))
     arrived = lax.all_to_all(blocks, "ell", split_axis=0, concat_axis=0, tiled=True)
     return total(arrived)

time: 74.3 us -> 69.9 us (0.941)
  local copies, waits for them, and re-layouts: 5.44 us -> 0.8 us
  waiting for transfers between devices: 2.66 us -> 7.08 us
  between operations: 2.01 us -> 0.03 us
  Pallas kernels: 27.2 us -> 25.8 us
    all_to_all x1, waiting for transfers between devices: 2.66 us -> 7.08 us  [body(): lax.all_to_all(sums.reshape(64, 3, 4, 128), 'ma', split_axis=0, concat_ax...]
    reshape x3 -> x0, local copies, waits for them, and re-layouts: 3.21 us -> none  [the longest x1 2.28 us: body(): harmonics.reshape(slots_here, 3, 8, columns_here)]
    dynamic_slice x2 -> x0, local copies, waits for them, and re-layouts: 1.35 us -> none  [the longest x1 0.76 us: body(): lax.dynamic_slice_in_dim(slot_orders, place * slots_here, slots_here)]
    pallas_call x1, Pallas kernels: 1.65 us -> 0.65 us  [total(): pl.pallas_call(total_kernel, in_specs=[vmem], out_specs=vmem, out_shape=j...]
    pallas_call x1, Pallas kernels: 8.91 us -> 8.07 us  [tables(): pl.pallas_call(tables_kernel, in_specs=[pl.BlockSpec(memory_space=pltpu.S...]
  transfers between devices with their start and end apart: 1 -> 1, of which waited for: 1 -> 1; matrix products, arithmetic and copies ran while one was open for 2% -> 0% of each run, Pallas kernels for 12% -> 12%
where the time goes in v2:
time: 69.9 us; the launch traced here: 69.5 us
  Pallas kernels  25.8 us (37%)
  blocking collectives  21 us (30%)
  starting transfers between devices  14.8 us (21%)
  waiting for transfers between devices  7.08 us (10%)
  local copies, waits for them, and re-layouts  0.8 us (1%)
    all_to_all x1, blocking collectives, body(): lax.all_to_all(blocks, 'ell', split_axis=0, concat_axis=0, tiled=True)  21 us
    all_to_all x1, starting transfers between devices, body(): lax.all_to_all(sums.reshape(64, 3, 4, 128), 'ma', split_axis=0, concat_ax...  14.8 us
    pallas_call x1, Pallas kernels, synthesis(): pl.pallas_call(synthesis_kernel, in_specs=[vmem, vmem, vmem, hbm, hbm, vm...  11.2 us
    pallas_call x1, Pallas kernels, tables(): pl.pallas_call(tables_kernel, in_specs=[pl.BlockSpec(memory_space=pltpu.S...  8.07 us
    all_to_all x1, waiting for transfers between devices, body(): lax.all_to_all(sums.reshape(64, 3, 4, 128), 'ma', split_axis=0, concat_ax...  7.08 us
    pallas_call x1, Pallas kernels, legendre_sums(): pl.pallas_call(legendre_kernel, grid_spec=pltpu.PrefetchScalarGridSpec(nu...  5.83 us
  transfers between devices with their start and end apart: 1, of which 1 were waited for; matrix products, arithmetic and copies ran while one was open for 0% of the time, Pallas kernels for 12%

profile of v2, /device:TPU:1, one launch (start us, length us, event | category | flops | bytes accessed | tf_op | source)
XLA Modules:
  0.0 69.5 jit_solution(10025564369499744147)
XLA Ops:
  0.0 5.8 %legendre_sums.1 = f32[768,128]{1,0:T(8,128)} custom-call(s32[2048]{0:T(1024)} %orders_ref.1, bf16[3,32,32,512]{3,2,1,0:T(8,128)(2,1)} %leg_ref.1, bf16[32,3,2,4,512]{4,3,2,1,0:T(4,128)(2,1)} %harm_ref.1), custom_call_target="tpu_custom_call" | custom-call | tf_op jit(solution)/shard_map/legendre_sums/pallas_call | solution.py:79
  5.8 14.8 %all-to-all-start = ((f32[64,3,4,128]{3,2,1,0:T(4,128)}), f32[64,3,4,128]{3,2,1,0:T(4,128)S(1)}, u32[]{:S(2)}, u32[]{:S(2)}) async-start(f32[64,3,4,128]{3,2,1,0:T(4,128)} %bitcast.4), calls=%async_computation | async-start | bytes 786432 | tf_op jit(solution)/shard_map/all_to_all | solution.py:305
  20.7 8.1 %tables.1 = (s32[16,128]{1,0:T(8,128)}, f32[2,16,16,128]{3,2,1,0:T(8,128)}, f32[2,16,16,128]{3,2,1,0:T(8,128)}, bf16[2,256,4096]{2,1,0:T(8,128)(2,1)}, bf16[2,256,4096]{2,1,0:T(8,128)(2,1)}) custom-call(s32[32]{0:T(128)} %cycle_ref.1, s32[16,128]{1,0:T(8,128)} %bitcast.5), custom_call_target="tpu_custom_call" | custom-call | tf_op jit(solution)/shard_map/tables/pallas_call | solution.py:177
  28.7 7.1 %all-to-all-done = f32[64,3,4,128]{3,2,1,0:T(4,128)S(1)} async-done(((f32[64,3,4,128]{3,2,1,0:T(4,128)}), f32[64,3,4,128]{3,2,1,0:T(4,128)S(1)}, u32[]{:S(2)}, u32[]{:S(2)}) %all-to-all-start) | async-done | bytes 393248 | tf_op jit(solution)/shard_map/all_to_all | solution.py:305
  35.8 0.0 copy-start
  35.8 0.8 %copy-done = f32[64,3,4,128]{3,2,1,0:T(4,128)} copy-done((f32[64,3,4,128]{3,2,1,0:T(4,128)}, f32[64,3,4,128]{3,2,1,0:T(4,128)S(1)}, u32[]{:S(2)}) %copy-start) | copy-done | bytes 393240
  36.6 11.2 %synthesis.1 = f32[8,48,256]{2,1,0:T(8,128)} custom-call(s32[16,128]{1,0:T(8,128)} %get-tuple-element.10.lower_ref, f32[2,16,16,128]{3,2,1,0:T(8,128)} %get-tuple-element.11.cos_ref, f32[2,16,16,128]{3,2,1,0:T(8,128)} %get-tuple-element.12.sin_ref, bf16[2,256,4096]{2,1,0:T(8,128)(2,1)} %get-tuple-element.13.high_ref, ...), custom_call_target="tpu_custom_call" | custom-call | tf_op jit(solution)/shard_map/synthesis/pallas_call | solution.py:260
  47.9 21.0 %all_to_all.10.parts_ref = f32[8,48,256]{2,1,0:T(8,128)S(1)} all-to-all(f32[8,48,256]{2,1,0:T(8,128)} %synthesis.1), channel_id=1, replica_groups=mesh['ma'=64,'ell'=8] {'ell'}, dimensions={0} | all-to-all | bytes 786432 | tf_op jit(solution)/shard_map/all_to_all | solution.py:308
  68.9 0.7 total.1
Async XLA Ops:
  5.8 30.0 %all-to-all-start = ((f32[64,3,4,128]{3,2,1,0:T(4,128)}), f32[64,3,4,128]{3,2,1,0:T(4,128)S(1)}, u32[]{:S(2)}, u32[]{:S(2)}) async-start(f32[64,3,4,128]{3,2,1,0:T(4,128)} %bitcast.4), calls=%async_computation | async-start | bytes 786432 | tf_op jit(solution)/shard_map/all_to_all | solution.py:305
  35.8 0.8 %copy-start = (f32[64,3,4,128]{3,2,1,0:T(4,128)}, f32[64,3,4,128]{3,2,1,0:T(4,128)S(1)}, u32[]{:S(2)}) copy-start(f32[64,3,4,128]{3,2,1,0:T(4,128)S(1)} %all-to-all-done) | copy-start | bytes 1179652

commit v3 on v2

--- a/solution.py
+++ b/solution.py
@@ -78,19 +78,17 @@
     slots, pairs, width = legendre.shape[1:]
     return pl.pallas_call(
         legendre_kernel,
-        grid_spec=pltpu.PrefetchScalarGridSpec(
-            num_scalar_prefetch=1,
-            grid=(slots // 8,),
-            in_specs=[
-                pl.BlockSpec((3, 8, pairs, width), lambda g, o: (0, g, 0, 0)),
-                pl.BlockSpec((8, 3, 2, 4, width), lambda g, o: (g, 0, 0, 0, 0)),
-            ],
-            out_specs=pl.BlockSpec((2 * pairs * 12, 128), lambda g, o: (0, 0)),
-            scratch_shapes=[
-                pltpu.VMEM((8, 96, 2 * width), BF16),
-                pltpu.VMEM((6, pairs, 128), F32),
-            ],
-        ),
+        grid=(slots // 8,),
+        in_specs=[
+            pl.BlockSpec(memory_space=pltpu.SMEM),
+            pl.BlockSpec((3, 8, pairs, width), lambda g: (0, g, 0, 0)),
+            pl.BlockSpec((8, 3, 2, 4, width), lambda g: (g, 0, 0, 0, 0)),
+        ],
+        out_specs=pl.BlockSpec((2 * pairs * 12, 128), lambda g: (0, 0)),
+        scratch_shapes=[
+            pltpu.VMEM((8, 96, 2 * width), BF16),
+            pltpu.VMEM((6, pairs, 128), F32),
+        ],
         out_shape=jax.ShapeDtypeStruct((2 * pairs * 12, 128), F32),
         name="legendre_sums",
     )(orders, legendre, harmonics)
@@ -115,8 +113,8 @@
     return high, (value - high.astype(F32)).astype(BF16)
 
 
-def tables_kernel(cycle_ref, slots_ref, lower_ref, cos_ref, sin_ref, high_ref, low_ref, high_buf, low_buf, sem):
-    slots = high_ref.shape[2] // 2
+def tables_kernel(cycle_ref, slots_ref, lower_ref, cos_ref, sin_ref, table_ref, table_buf, sem):
+    slots = table_ref.shape[3]
     tiles = slots // 128
     shift = cycle_ref[lax.axis_index("ma") % cycle_ref.shape[0]] % 2
     row = lax.broadcasted_iota(jnp.int32, (16, 128), 0)
@@ -133,25 +131,22 @@
     def one_tile(tile):
         lower = lower_ref[pl.ds(tile, 1), :]
         odd = lower % 2
-        lanes = pl.multiple_of(tile * 128, 128)
+        lanes = pl.ds(pl.multiple_of(tile * 128, 128), 128)
         for parity in range(2):
             order = jnp.where(odd == parity, lower, 4095 - lower)
             factor = jnp.where(order == 0, 1.0, 2.0).astype(F32)
-            cosine, sine = cos_sin((order * (512 * row + shift)) & 16383)
+            cosine, sine = cos_sin((order * (512 * row + (255 + shift))) & 16383)
             cos_ref[parity, tile] = cosine * factor
             sin_ref[parity, tile] = sine * factor
-            cos_v, sin_v = cos_sin((order * (2 * row)) & 16383)
-            cos_u, sin_u = cos_sin((order * (32 * row)) & 16383)
-            for u in range(16):
+            cos_v, sin_v = cos_sin((order * (2 * row + 1)) & 16383)
+            cos_u, sin_u = cos_sin((order * (32 * row[0:8])) & 16383)
+            for u in range(8):
                 cu = cos_u[u : u + 1, :]
                 su = sin_u[u : u + 1, :]
-                pixels = slice(16 * u, 16 * u + 16)
-                high, low = high_low(cu * cos_v - su * sin_v)
-                high_buf[parity, pixels, pl.ds(lanes, 128)] = high
-                low_buf[parity, pixels, pl.ds(lanes, 128)] = low
-                high, low = high_low(su * cos_v + cu * sin_v)
-                high_buf[parity, pixels, pl.ds(slots + lanes, 128)] = high
-                low_buf[parity, pixels, pl.ds(slots + lanes, 128)] = low
+                for part, value in enumerate((cu * cos_v - su * sin_v, su * cos_v + cu * sin_v)):
+                    high, low = high_low(value)
+                    table_buf[parity, part, 16 * u : 16 * u + 16, lanes] = high
+                    table_buf[parity, part, 128 + 16 * u : 144 + 16 * u, lanes] = low
 
     copies = []
     span = 4
@@ -159,11 +154,10 @@
         pl.loop(block * span, (block + 1) * span)(one_tile)
         for parity in range(2):
             for part in range(2):
-                for buf, ref in ((high_buf, high_ref), (low_buf, low_ref)):
-                    view = (parity, slice(None), pl.ds(part * slots + block * span * 128, span * 128))
-                    copy = pltpu.make_async_copy(buf.at[view], ref.at[view], sem.at[len(copies)])
-                    copy.start()
-                    copies.append(copy)
+                view = (parity, part, slice(None), pl.ds(block * span * 128, span * 128))
+                copy = pltpu.make_async_copy(table_buf.at[view], table_ref.at[view], sem.at[len(copies)])
+                copy.start()
+                copies.append(copy)
     for copy in copies:
         copy.wait()
 
@@ -173,37 +167,33 @@
     vmem = pl.BlockSpec(memory_space=pltpu.VMEM)
     hbm = pl.BlockSpec(memory_space=pltpu.HBM)
     small = jax.ShapeDtypeStruct((2, slots // 128, 16, 128), F32)
-    large = jax.ShapeDtypeStruct((2, 256, 2 * slots), BF16)
     return pl.pallas_call(
         tables_kernel,
         in_specs=[pl.BlockSpec(memory_space=pltpu.SMEM), vmem],
-        out_specs=[vmem, vmem, vmem, hbm, hbm],
-        out_shape=[jax.ShapeDtypeStruct((slots // 128, 128), jnp.int32), small, small, large, large],
+        out_specs=[vmem, vmem, vmem, hbm],
+        out_shape=[
+            jax.ShapeDtypeStruct((slots // 128, 128), jnp.int32),
+            small,
+            small,
+            jax.ShapeDtypeStruct((2, 2, 256, slots), BF16),
+        ],
         scratch_shapes=[
-            pltpu.VMEM((2, 256, 2 * slots), BF16),
-            pltpu.VMEM((2, 256, 2 * slots), BF16),
-            pltpu.SemaphoreType.DMA((slots // 64,)),
-        ],
-        compiler_params=pltpu.CompilerParams(vmem_limit_bytes=60 << 20),
+            pltpu.VMEM((2, 2, 256, slots), BF16),
+            pltpu.SemaphoreType.DMA((slots // 128,)),
+        ],
+        compiler_params=pltpu.CompilerParams(vmem_limit_bytes=52 << 20),
         name="tables",
     )(cycle_index, slot_orders.reshape(slots // 128, 128))
 
 
-def synthesis_kernel(
-    lower_ref, cos_ref, sin_ref, high_ref, low_ref, sums_ref, out_ref, x_ref, a_ref, high_buf, low_buf, sem
-):
-    slots = high_ref.shape[2] // 2
+def synthesis_kernel(lower_ref, cos_ref, sin_ref, table_ref, sums_ref, out_ref, x_ref, a_ref, table_buf, sem):
+    slots = table_ref.shape[3]
     tiles = slots // 128
     copies = [
-        [
-            pltpu.make_async_copy(ref.at[parity], buf.at[parity], sem.at[2 * parity + i])
-            for i, (ref, buf) in enumerate(((high_ref, high_buf), (low_ref, low_buf)))
-        ]
-        for parity in range(2)
+        pltpu.make_async_copy(table_ref.at[parity], table_buf.at[parity], sem.at[parity]) for parity in range(2)
     ]
-    for pair in copies:
-        for copy in pair:
-            copy.start()
+    for copy in copies:
+        copy.start()
     for field in range(3):
         for pair in range(2):
             pieces = []
@@ -217,7 +207,7 @@
     @pl.loop(0, tiles)
     def _(tile):
         odd = (lower_ref[pl.ds(tile, 1), :] % 2) == 1
-        lanes = pl.multiple_of(tile * 128, 128)
+        lanes = pl.ds(pl.multiple_of(tile * 128, 128), 128)
         for field in range(3):
             x = x_ref[field, tile]
             for parity in range(2):
@@ -229,56 +219,62 @@
                     real = chosen[comp : comp + 1, :]
                     imag = chosen[4 + comp : 5 + comp, :]
                     rows = (field * 4 + comp) * 16
-                    high, low = high_low(real * cosine - imag * sine)
-                    a_ref[parity, rows : rows + 16, pl.ds(lanes, 128)] = high
-                    a_ref[parity, 192 + rows : 208 + rows, pl.ds(lanes, 128)] = low
-                    high, low = high_low(-(real * sine + imag * cosine))
-                    a_ref[parity, rows : rows + 16, pl.ds(slots + lanes, 128)] = high
-                    a_ref[parity, 192 + rows : 208 + rows, pl.ds(slots + lanes, 128)] = low
-
-    parts = []
+                    for part, value in enumerate(
+                        (real * cosine - imag * sine, -(real * sine + imag * cosine))
+                    ):
+                        high, low = high_low(value)
+                        a_ref[parity, part, rows : rows + 16, lanes] = high
+                        a_ref[parity, part, 192 + rows : 208 + rows, lanes] = low
+
+    sides = []
     for parity in range(2):
-        for copy in copies[parity]:
-            copy.wait()
-        wide = lax.dot_general(a_ref[parity], high_buf[parity], NT, preferred_element_type=F32)
-        fine = lax.dot_general(a_ref[parity, 0:192, :], low_buf[parity], NT, preferred_element_type=F32)
-        parts.append(wide[0:192] + (wide[192:384] + fine))
-    near = parts[0] + parts[1]
-    far = parts[0] - parts[1]
-    for block in range(4):
-        for row in range(12):
-            place = slice(row * 4, row * 4 + 4)
-            source = slice(row * 16 + block * 4, row * 16 + block * 4 + 4)
-            out_ref[block, place, :] = near[source, :]
-            out_ref[block + 4, place, :] = far[source, :]
-
-
-def synthesis(lower, cosine, sine, high, low, sums):
+        copies[parity].wait()
+        both = []
+        for part in range(2):
+            wide = lax.dot_general(
+                a_ref[parity, part], table_buf[parity, part], NT, preferred_element_type=F32
+            )
+            fine = wide[0:192, 128:256] + wide[192:384, 128:256]
+            both.append(wide[0:192, 0:128] + (wide[192:384, 0:128] + fine))
+        sides.append((both[0] - both[1], both[0] + both[1]))
+    for side in range(2):
+        lanes = slice(side * 128, side * 128 + 128)
+        near = sides[0][side] + sides[1][side]
+        far = sides[0][side] - sides[1][side]
+        for block in range(4):
+            for row in range(12):
+                place = slice(row * 4, row * 4 + 4)
+                source = slice(row * 16 + block * 4, row * 16 + block * 4 + 4)
+                out_ref[block, place, lanes] = near[source, :]
+                out_ref[block + 4, place, lanes] = far[source, :]
+
+
+def synthesis(lower, cosine, sine, table, sums):
     vmem = pl.BlockSpec(memory_space=pltpu.VMEM)
     hbm = pl.BlockSpec(memory_space=pltpu.HBM)
-    slots = high.shape[2] // 2
+    slots = table.shape[3]
     return pl.pallas_call(
         synthesis_kernel,
-        in_specs=[vmem, vmem, vmem, hbm, hbm, vmem],
+        in_specs=[vmem, vmem, vmem, hbm, vmem],
         out_specs=vmem,
         out_shape=jax.ShapeDtypeStruct((8, 48, 256), F32),
         scratch_shapes=[
             pltpu.VMEM((3, slots // 128, 16, 128), F32),
-            pltpu.VMEM((2, 384, 2 * slots), BF16),
-            pltpu.VMEM((2, 256, 2 * slots), BF16),
-            pltpu.VMEM((2, 256, 2 * slots), BF16),
-            pltpu.SemaphoreType.DMA((4,)),
-        ],
-        compiler_params=pltpu.CompilerParams(vmem_limit_bytes=60 << 20),
+            pltpu.VMEM((2, 2, 384, slots), BF16),
+            pltpu.VMEM((2, 2, 256, slots), BF16),
+            pltpu.SemaphoreType.DMA((2,)),
+        ],
+        compiler_params=pltpu.CompilerParams(vmem_limit_bytes=52 << 20),
         name="synthesis",
-    )(lower, cosine, sine, high, low, sums)
+    )(lower, cosine, sine, table, sums)
 
 
 def total_kernel(parts_ref, out_ref, sum_ref):
     total = parts_ref[0]
     for source in range(1, 8):
         total = total + parts_ref[source]
-    sum_ref[0] = total[:, 0:128]
+    falling = 127 - lax.broadcasted_iota(jnp.int32, (48, 128), 1)
+    sum_ref[0] = jnp.take_along_axis(total[:, 0:128], falling, axis=1)
     sum_ref[1] = total[:, 128:256]
     for field in range(3):
         for piece in range(4):
@@ -303,8 +299,8 @@
 def body(legendre, harmonics, slot_orders, cycle_index):
     sums = legendre_sums(legendre, harmonics, slot_orders)
     moved = lax.all_to_all(sums.reshape(64, 3, 4, 128), "ma", split_axis=0, concat_axis=0, tiled=True)
-    lower, cosine, sine, high, low = tables(cycle_index, slot_orders)
-    blocks = synthesis(lower, cosine, sine, high, low, moved.reshape(768, 128))
+    lower, cosine, sine, table = tables(cycle_index, slot_orders)
+    blocks = synthesis(lower, cosine, sine, table, moved.reshape(768, 128))
     arrived = lax.all_to_all(blocks, "ell", split_axis=0, concat_axis=0, tiled=True)
     return total(arrived)
 

time: 69.9 us -> 61.2 us (0.88)
  Pallas kernels: 25.8 us -> 14.5 us
  waiting for transfers between devices: 7.08 us -> 10.8 us
  local copies, waits for them, and re-layouts: 0.8 us -> 0.01 us
    pallas_call x2, Pallas kernels: 17 us -> 9.47 us  [the longest x1 5.02 us: legendre_sums(): pl.pallas_call(legendre_kernel, grid=(slots // 8,), in_specs=[pl.BlockSpe...]
    pallas_call x1, Pallas kernels: 8.07 us -> 4.32 us  [tables(): pl.pallas_call(tables_kernel, in_specs=[pl.BlockSpec(memory_space=pltpu.S...]
    all_to_all x1, waiting for transfers between devices: 7.08 us -> 10.8 us  [body(): lax.all_to_all(sums.reshape(64, 3, 4, 128), 'ma', split_axis=0, concat_ax...]
    unnamed x2 -> x4, local copies, waits for them, and re-layouts: 0.8 us -> 0.01 us
  transfers between devices with their start and end apart: 1 -> 1, of which waited for: 1 -> 1; matrix products, arithmetic and copies ran while one was open for 0% -> 0% of each run, Pallas kernels for 12% -> 7%
where the time goes in v3:
time: 61.2 us; the launch traced here: 61 us
  blocking collectives  20.8 us (34%)
  starting transfers between devices  14.8 us (24%)
  Pallas kernels  14.5 us (24%)
  waiting for transfers between devices  10.8 us (18%)
    all_to_all x1, blocking collectives, body(): lax.all_to_all(blocks, 'ell', split_axis=0, concat_axis=0, tiled=True)  20.8 us
    all_to_all x1, starting transfers between devices, body(): lax.all_to_all(sums.reshape(64, 3, 4, 128), 'ma', split_axis=0, concat_ax...  14.8 us
    all_to_all x1, waiting for transfers between devices, body(): lax.all_to_all(sums.reshape(64, 3, 4, 128), 'ma', split_axis=0, concat_ax...  10.8 us
    pallas_call x1, Pallas kernels, legendre_sums(): pl.pallas_call(legendre_kernel, grid=(slots // 8,), in_specs=[pl.BlockSpe...  5.02 us
    pallas_call x1, Pallas kernels, synthesis(): pl.pallas_call(synthesis_kernel, in_specs=[vmem, vmem, vmem, hbm, vmem],...  4.45 us
    pallas_call x1, Pallas kernels, tables(): pl.pallas_call(tables_kernel, in_specs=[pl.BlockSpec(memory_space=pltpu.S...  4.32 us
  transfers between devices with their start and end apart: 1, of which 1 were waited for; matrix products, arithmetic and copies ran while one was open for 0% of the time, Pallas kernels for 7%

profile of v3, /device:TPU:1, one launch (start us, length us, event | category | flops | bytes accessed | tf_op | source)
XLA Modules:
  0.0 61.0 jit_solution(6179357995176639589)
XLA Ops:
  0.0 0.0 copy-start
  0.0 0.0 copy-start.1
  0.0 5.0 %legendre_sums.1 = f32[768,128]{1,0:T(8,128)} custom-call(s32[2048]{0:T(1024)} %orders_ref.1, bf16[3,32,32,512]{3,2,1,0:T(8,128)(2,1)} %leg_ref.1, bf16[32,3,2,4,512]{4,3,2,1,0:T(4,128)(2,1)} %harm_ref.1), custom_call_target="tpu_custom_call" | custom-call | tf_op jit(solution)/shard_map/legendre_sums/pallas_call | solution.py:79
  5.0 14.8 %all-to-all-start = ((f32[64,3,4,128]{3,2,1,0:T(4,128)}), f32[64,3,4,128]{3,2,1,0:T(4,128)S(1)}, u32[]{:S(2)}, u32[]{:S(2)}) async-start(f32[64,3,4,128]{3,2,1,0:T(4,128)} %bitcast.5), calls=%async_computation | async-start | bytes 786432 | tf_op jit(solution)/shard_map/all_to_all | solution.py:301
  19.9 0.0 copy-done
  19.9 0.0 copy-done.1
  19.9 4.3 %tables.1 = (s32[16,128]{1,0:T(8,128)S(1)}, f32[2,16,16,128]{3,2,1,0:T(8,128)S(1)}, f32[2,16,16,128]{3,2,1,0:T(8,128)S(1)}, bf16[2,2,256,2048]{3,2,1,0:T(8,128)(2,1)}) custom-call(s32[32]{0:T(128)S(1)} %copy-done.1, s32[16,128]{1,0:T(8,128)S(1)} %bitcast.4), custom_call_target="tpu_custom_call" | custom-call | tf_op jit(solution)/shard_map/tables/pallas_call | solution.py:170
  24.2 10.8 %all-to-all-done = f32[64,3,4,128]{3,2,1,0:T(4,128)S(1)} async-done(((f32[64,3,4,128]{3,2,1,0:T(4,128)}), f32[64,3,4,128]{3,2,1,0:T(4,128)S(1)}, u32[]{:S(2)}, u32[]{:S(2)}) %all-to-all-start) | async-done | bytes 393248 | tf_op jit(solution)/shard_map/all_to_all | solution.py:301
  35.0 4.5 %synthesis.1 = f32[8,48,256]{2,1,0:T(8,128)S(1)} custom-call(s32[16,128]{1,0:T(8,128)S(1)} %get-tuple-element.9.lower_ref, f32[2,16,16,128]{3,2,1,0:T(8,128)S(1)} %get-tuple-element.10.cos_ref, f32[2,16,16,128]{3,2,1,0:T(8,128)S(1)} %get-tuple-element.11.sin_ref, bf16[2,2,256,2048]{3,2,1,0:T(8,128)(2,1)} %get-tuple-element.12.table_ref, f32[768,128]{1,0:T(8,128)S(1)} %bitcast.3), custom_call_target="tpu_custom_call" | custom-call | tf_op jit(solution)/shard_map/synthesis/pallas_call | solution.py:256
  39.5 20.8 %all_to_all.10.parts_ref = f32[8,48,256]{2,1,0:T(8,128)S(1)} all-to-all(f32[8,48,256]{2,1,0:T(8,128)S(1)} %synthesis.1), channel_id=1, replica_groups=mesh['ma'=64,'ell'=8] {'ell'}, dimensions={0} | all-to-all | bytes 786432 | tf_op jit(solution)/shard_map/all_to_all | solution.py:304
  60.3 0.7 %total.1 = f32[1,3,4,1024]{3,2,1,0:T(4,128)} custom-call(f32[8,48,256]{2,1,0:T(8,128)S(1)} %all_to_all.10.parts_ref), custom_call_target="tpu_custom_call" | custom-call | tf_op jit(solution)/shard_map/total/pallas_call | solution.py:288
Async XLA Ops:
  0.0 19.9 %copy-start = (s32[2048]{0:T(1024)S(1)}, s32[2048]{0:T(1024)}, u32[]{:S(2)}) copy-start(s32[2048]{0:T(1024)} %orders_ref.1) | copy-start | bytes 24580
  0.0 19.9 %copy-start.1 = (s32[32]{0:T(128)S(1)}, s32[32]{0:T(128)}, u32[]{:S(2)}) copy-start(s32[32]{0:T(128)} %cycle_ref.1) | copy-start | bytes 388
  5.0 30.0 %all-to-all-start = ((f32[64,3,4,128]{3,2,1,0:T(4,128)}), f32[64,3,4,128]{3,2,1,0:T(4,128)S(1)}, u32[]{:S(2)}, u32[]{:S(2)}) async-start(f32[64,3,4,128]{3,2,1,0:T(4,128)} %bitcast.5), calls=%async_computation | async-start | bytes 786432 | tf_op jit(solution)/shard_map/all_to_all | solution.py:301

commit v4 on v3

--- a/solution.py
+++ b/solution.py
@@ -12,9 +12,36 @@
 NT = (((1,), (1,)), ((), ()))
 
 
-def legendre_kernel(orders_ref, leg_ref, harm_ref, out_ref, pack_ref, acc_ref):
-    group = pl.program_id(0)
-    groups = pl.num_programs(0)
+def legendre_kernel(
+    orders_hbm, leg_hbm, harm_hbm, out_ref, orders_ref, leg_all, harm_all, pack_ref, acc_ref, sem, orders_sem
+):
+    groups = leg_hbm.shape[1] // 8
+    orders_copy = pltpu.make_async_copy(orders_hbm, orders_ref, orders_sem)
+    orders_copy.start()
+
+    def arrivals(group):
+        span = pl.ds(group * 8, 8)
+        return (
+            pltpu.make_async_copy(harm_hbm.at[span], harm_all.at[span], sem.at[0, group]),
+            pltpu.make_async_copy(leg_hbm.at[:, span], leg_all.at[:, span], sem.at[1, group]),
+        )
+
+    for group in range(groups):
+        for copy in arrivals(group):
+            copy.start()
+    orders_copy.wait()
+
+    @pl.loop(0, groups)
+    def _(group):
+        for copy in arrivals(group):
+            copy.wait()
+        span = pl.ds(group * 8, 8)
+        legendre_group(
+            group, groups, orders_ref, leg_all.at[:, span], harm_all.at[span], out_ref, pack_ref, acc_ref
+        )
+
+
+def legendre_group(group, groups, orders_ref, leg_ref, harm_ref, out_ref, pack_ref, acc_ref):
     pairs = leg_ref.shape[2]
     width = leg_ref.shape[3]
     full = 2 * orders_ref.shape[0]
@@ -22,43 +49,43 @@
     column = lax.axis_index("ell") * width + lax.broadcasted_iota(jnp.int32, (1, width), 1)
     column_sign = (1 - 2 * (column % 2)).astype(F32)
     half = lax.broadcasted_iota(jnp.int32, (8, width), 0) < 4
+    upper_rows = lax.broadcasted_iota(jnp.int32, (16, width), 0) >= 8
     for slot in range(8):
         lower = orders_ref[first_slot + slot]
         boundary = full - 1 - lower
-        lower_part = jnp.where(column < boundary, 1.0, 0.0).astype(F32)
-        upper_part = jnp.where((column >= boundary) & (column < full - 1), 1.0, 0.0).astype(F32)
-        upper_sign = column_sign * (2 * (lower % 2) - 1).astype(F32)
+        past = column >= boundary
+        inside = (column < full - 1) & (past == upper_rows)
+        weights = jnp.where(inside, 1.0, 0.0).astype(F32)
+        flips = column_sign * jnp.where(upper_rows, (2 * (lower % 2) - 1).astype(F32), 1.0)
+        signed = weights * flips
         temp, emode, bmode = (
             jnp.concatenate([harm_ref[slot, kind, part].astype(F32) for part in range(2)], axis=0)
             for kind in range(3)
         )
         eturn = pltpu.roll(emode, 4, 0)
-        eturn = jnp.where(half, eturn, -eturn)
+        eturn = jnp.where(half, -eturn, eturn)
         bturn = pltpu.roll(bmode, 4, 0)
         bturn = jnp.where(half, bturn, -bturn)
+
+        def twice(values):
+            return jnp.concatenate([values, values], axis=0).astype(BF16)
+
+        temp, emode, bmode = twice(temp), twice(-emode), twice(-bmode)
+        eturn, bturn = twice(eturn), twice(bturn)
         for side in range(2):
-            if side == 0:
-                weights = (lower_part, upper_part)
-                turned = weights
-            else:
-                weights = (lower_part * column_sign, upper_part * upper_sign)
-                turned = (-weights[0], -weights[1])
-
-            def rows(values, scales):
-                return jnp.concatenate([values * scales[0], values * scales[1]], axis=0).astype(BF16)
-
-            minus = (-weights[0], -weights[1])
-            straight = (-turned[0], -turned[1])
+            straight = (signed if side else weights).astype(BF16)
+            turned = (-signed).astype(BF16) if side else straight
             base = side * 32
-            pack_ref[slot, base : base + 16, 0:width] = rows(emode, minus)
-            pack_ref[slot, base : base + 16, width : 2 * width] = rows(bturn, turned)
-            pack_ref[slot, base + 16 : base + 32, 0:width] = rows(bmode, minus)
-            pack_ref[slot, base + 16 : base + 32, width : 2 * width] = rows(eturn, straight)
-            pack_ref[slot, 64 + side * 16 : 80 + side * 16, 0:width] = rows(temp, weights)
+            pack_ref[slot, base : base + 16, 0:width] = emode * straight
+            pack_ref[slot, base : base + 16, width : 2 * width] = bturn * turned
+            pack_ref[slot, base + 16 : base + 32, 0:width] = bmode * straight
+            pack_ref[slot, base + 16 : base + 32, width : 2 * width] = eturn * turned
+            pack_ref[slot, 64 + side * 16 : 80 + side * 16, 0:width] = temp * straight
         both = lax.dot_general(
-            leg_ref[1, slot], pack_ref[slot, 0:64, 0:width], NT, preferred_element_type=F32
-        ) + lax.dot_general(
-            leg_ref[2, slot], pack_ref[slot, 0:64, width : 2 * width], NT, preferred_element_type=F32
+            jnp.concatenate([leg_ref[1, slot], leg_ref[2, slot]], axis=1),
+            pack_ref[slot, 0:64],
+            NT,
+            preferred_element_type=F32,
         )
         plain = lax.dot_general(
             leg_ref[0, slot], pack_ref[slot, 64:96, 0:width], NT, preferred_element_type=F32
@@ -78,16 +105,16 @@
     slots, pairs, width = legendre.shape[1:]
     return pl.pallas_call(
         legendre_kernel,
-        grid=(slots // 8,),
-        in_specs=[
-            pl.BlockSpec(memory_space=pltpu.SMEM),
-            pl.BlockSpec((3, 8, pairs, width), lambda g: (0, g, 0, 0)),
-            pl.BlockSpec((8, 3, 2, 4, width), lambda g: (g, 0, 0, 0, 0)),
-        ],
-        out_specs=pl.BlockSpec((2 * pairs * 12, 128), lambda g: (0, 0)),
+        in_specs=[pl.BlockSpec(memory_space=pltpu.HBM)] * 3,
+        out_specs=pl.BlockSpec(memory_space=pltpu.VMEM),
         scratch_shapes=[
+            pltpu.SMEM(orders.shape, jnp.int32),
+            pltpu.VMEM((3, slots, pairs, width), BF16),
+            pltpu.VMEM(harmonics.shape, BF16),
             pltpu.VMEM((8, 96, 2 * width), BF16),
             pltpu.VMEM((6, pairs, 128), F32),
+            pltpu.SemaphoreType.DMA((2, slots // 8)),
+            pltpu.SemaphoreType.DMA,
         ],
         out_shape=jax.ShapeDtypeStruct((2 * pairs * 12, 128), F32),
         name="legendre_sums",
@@ -202,22 +229,23 @@
                     start = device * 12 + field * 4 + pair * 2 + middle
                     pieces.append(sums_ref[pl.ds(start, 16, stride=48), :])
             turned = jnp.concatenate(pieces, axis=0).T
-            x_ref[field, pair * 8 : pair * 8 + 8] = turned.reshape(8, 16, 128)
+            turned = turned.reshape(8, 16, 128)
+            odd = (lower_ref[pair * 8 : pair * 8 + 8, :] % 2 == 1)[:, None, :]
+            x_ref[0, field, pair * 8 : pair * 8 + 8] = jnp.where(odd, turned[:, 8:16], turned[:, 0:8])
+            x_ref[1, field, pair * 8 : pair * 8 + 8] = jnp.where(odd, turned[:, 0:8], turned[:, 8:16])
 
     @pl.loop(0, tiles)
     def _(tile):
-        odd = (lower_ref[pl.ds(tile, 1), :] % 2) == 1
         lanes = pl.ds(pl.multiple_of(tile * 128, 128), 128)
-        for field in range(3):
-            x = x_ref[field, tile]
-            for parity in range(2):
-                keep = odd if parity else jnp.logical_not(odd)
-                chosen = jnp.where(keep, x[0:8], x[8:16])
-                cosine = cos_ref[parity, tile]
-                sine = sin_ref[parity, tile]
+
+        @pl.loop(0, 2)
+        def _(parity):
+            cosine = cos_ref[parity, tile]
+            sine = sin_ref[parity, tile]
+            for field in range(3):
                 for comp in range(4):
-                    real = chosen[comp : comp + 1, :]
-                    imag = chosen[4 + comp : 5 + comp, :]
+                    real = x_ref[parity, field, tile, pl.ds(comp, 16, stride=0), :]
+                    imag = x_ref[parity, field, tile, pl.ds(4 + comp, 16, stride=0), :]
                     rows = (field * 4 + comp) * 16
                     for part, value in enumerate(
                         (real * cosine - imag * sine, -(real * sine + imag * cosine))
@@ -259,7 +287,7 @@
         out_specs=vmem,
         out_shape=jax.ShapeDtypeStruct((8, 48, 256), F32),
         scratch_shapes=[
-            pltpu.VMEM((3, slots // 128, 16, 128), F32),
+            pltpu.VMEM((2, 3, slots // 128, 8, 128), F32),
             pltpu.VMEM((2, 2, 384, slots), BF16),
             pltpu.VMEM((2, 2, 256, slots), BF16),
             pltpu.SemaphoreType.DMA((2,)),

time: 61.2 us -> 60.6 us (level)
  no operation moved by 1% of the time
where the time goes in v4:
time: 60.6 us; the launch traced here: 60.5 us
  blocking collectives  20.8 us (34%)
  starting transfers between devices  14.8 us (24%)
  Pallas kernels  13.9 us (23%)
  waiting for transfers between devices  10.8 us (18%)
    all_to_all x1, blocking collectives, body(): lax.all_to_all(blocks, 'ell', split_axis=0, concat_axis=0, tiled=True)  20.8 us
    all_to_all x1, starting transfers between devices, body(): lax.all_to_all(sums.reshape(64, 3, 4, 128), 'ma', split_axis=0, concat_ax...  14.8 us
    all_to_all x1, waiting for transfers between devices, body(): lax.all_to_all(sums.reshape(64, 3, 4, 128), 'ma', split_axis=0, concat_ax...  10.8 us
    pallas_call x1, Pallas kernels, legendre_sums(): pl.pallas_call(legendre_kernel, in_specs=[pl.BlockSpec(memory_space=pltpu...  4.47 us
    pallas_call x1, Pallas kernels, synthesis(): pl.pallas_call(synthesis_kernel, in_specs=[vmem, vmem, vmem, hbm, vmem],...  4.43 us
    pallas_call x1, Pallas kernels, tables(): pl.pallas_call(tables_kernel, in_specs=[pl.BlockSpec(memory_space=pltpu.S...  4.32 us
  transfers between devices with their start and end apart: 1, of which 1 were waited for; matrix products, arithmetic and copies ran while one was open for 0% of the time, Pallas kernels for 7%

profile of v4, /device:TPU:1, one launch (start us, length us, event | category | flops | bytes accessed | tf_op | source)
XLA Modules:
  0.0 60.5 jit_solution(16571009968414275991)
XLA Ops:
  0.0 0.0 copy-start
  0.0 0.0 copy-start.1
  0.0 4.5 %legendre_sums.1 = f32[768,128]{1,0:T(8,128)} custom-call(s32[2048]{0:T(1024)} %orders_hbm.1, bf16[3,32,32,512]{3,2,1,0:T(8,128)(2,1)} %leg_hbm.1, bf16[32,3,2,4,512]{4,3,2,1,0:T(4,128)(2,1)} %harm_hbm.1), custom_call_target="tpu_custom_call" | custom-call | tf_op jit(solution)/shard_map/legendre_sums/pallas_call | solution.py:106
  4.5 14.8 %all-to-all-start = ((f32[64,3,4,128]{3,2,1,0:T(4,128)}), f32[64,3,4,128]{3,2,1,0:T(4,128)S(1)}, u32[]{:S(2)}, u32[]{:S(2)}) async-start(f32[64,3,4,128]{3,2,1,0:T(4,128)} %bitcast.5), calls=%async_computation | async-start | bytes 786432 | tf_op jit(solution)/shard_map/all_to_all | solution.py:329
  19.3 0.0 copy-done
  19.3 0.0 copy-done.1
  19.4 4.3 %tables.1 = (s32[16,128]{1,0:T(8,128)S(1)}, f32[2,16,16,128]{3,2,1,0:T(8,128)S(1)}, f32[2,16,16,128]{3,2,1,0:T(8,128)S(1)}, bf16[2,2,256,2048]{3,2,1,0:T(8,128)(2,1)}) custom-call(s32[32]{0:T(128)S(1)} %copy-done.1, s32[16,128]{1,0:T(8,128)S(1)} %bitcast.4), custom_call_target="tpu_custom_call" | custom-call | tf_op jit(solution)/shard_map/tables/pallas_call | solution.py:197
  23.7 10.8 %all-to-all-done = f32[64,3,4,128]{3,2,1,0:T(4,128)S(1)} async-done(((f32[64,3,4,128]{3,2,1,0:T(4,128)}), f32[64,3,4,128]{3,2,1,0:T(4,128)S(1)}, u32[]{:S(2)}, u32[]{:S(2)}) %all-to-all-start) | async-done | bytes 393248 | tf_op jit(solution)/shard_map/all_to_all | solution.py:329
  34.5 4.4 %synthesis.1 = f32[8,48,256]{2,1,0:T(8,128)S(1)} custom-call(s32[16,128]{1,0:T(8,128)S(1)} %get-tuple-element.9.lower_ref, f32[2,16,16,128]{3,2,1,0:T(8,128)S(1)} %get-tuple-element.10.cos_ref, f32[2,16,16,128]{3,2,1,0:T(8,128)S(1)} %get-tuple-element.11.sin_ref, bf16[2,2,256,2048]{3,2,1,0:T(8,128)(2,1)} %get-tuple-element.12.table_ref, f32[768,128]{1,0:T(8,128)S(1)} %bitcast.3), custom_call_target="tpu_custom_call" | custom-call | tf_op jit(solution)/shard_map/synthesis/pallas_call | solution.py:284
  38.9 20.8 %all_to_all.10.parts_ref = f32[8,48,256]{2,1,0:T(8,128)S(1)} all-to-all(f32[8,48,256]{2,1,0:T(8,128)S(1)} %synthesis.1), channel_id=1, replica_groups=mesh['ma'=64,'ell'=8] {'ell'}, dimensions={0} | all-to-all | bytes 786432 | tf_op jit(solution)/shard_map/all_to_all | solution.py:332
  59.7 0.7 %total.1 = f32[1,3,4,1024]{3,2,1,0:T(4,128)} custom-call(f32[8,48,256]{2,1,0:T(8,128)S(1)} %all_to_all.10.parts_ref), custom_call_target="tpu_custom_call" | custom-call | tf_op jit(solution)/shard_map/total/pallas_call | solution.py:316
Async XLA Ops:
  0.0 19.3 %copy-start = (s32[2048]{0:T(1024)S(1)}, s32[2048]{0:T(1024)}, u32[]{:S(2)}) copy-start(s32[2048]{0:T(1024)} %orders_hbm.1) | copy-start | bytes 24580
  0.0 19.3 %copy-start.1 = (s32[32]{0:T(128)S(1)}, s32[32]{0:T(128)}, u32[]{:S(2)}) copy-start(s32[32]{0:T(128)} %cycle_ref.1) | copy-start | bytes 388
  4.5 30.0 %all-to-all-start = ((f32[64,3,4,128]{3,2,1,0:T(4,128)}), f32[64,3,4,128]{3,2,1,0:T(4,128)S(1)}, u32[]{:S(2)}, u32[]{:S(2)}) async-start(f32[64,3,4,128]{3,2,1,0:T(4,128)} %bitcast.5), calls=%async_computation | async-start | bytes 786432 | tf_op jit(solution)/shard_map/all_to_all | solution.py:329

commit v5 on v4

--- a/solution.py
+++ b/solution.py
@@ -164,7 +164,7 @@
             factor = jnp.where(order == 0, 1.0, 2.0).astype(F32)
             cosine, sine = cos_sin((order * (512 * row + (255 + shift))) & 16383)
             cos_ref[parity, tile] = cosine * factor
-            sin_ref[parity, tile] = sine * factor
+            sin_ref[parity, tile] = -sine * factor
             cos_v, sin_v = cos_sin((order * (2 * row + 1)) & 16383)
             cos_u, sin_u = cos_sin((order * (32 * row[0:8])) & 16383)
             for u in range(8):
@@ -217,7 +217,10 @@
     slots = table_ref.shape[3]
     tiles = slots // 128
     copies = [
-        pltpu.make_async_copy(table_ref.at[parity], table_buf.at[parity], sem.at[parity]) for parity in range(2)
+        pltpu.make_async_copy(
+            table_ref.at[parity], table_buf.at[parity, :, :, pl.ds(0, slots)], sem.at[parity]
+        )
+        for parity in range(2)
     ]
     for copy in copies:
         copy.start()
@@ -238,18 +241,17 @@
     def _(tile):
         lanes = pl.ds(pl.multiple_of(tile * 128, 128), 128)
 
-        @pl.loop(0, 2)
+        @pl.loop(0, 2, unroll=2)
         def _(parity):
             cosine = cos_ref[parity, tile]
-            sine = sin_ref[parity, tile]
+            minus = sin_ref[parity, tile]
             for field in range(3):
+                x = x_ref[parity, field, tile]
                 for comp in range(4):
-                    real = x_ref[parity, field, tile, pl.ds(comp, 16, stride=0), :]
-                    imag = x_ref[parity, field, tile, pl.ds(4 + comp, 16, stride=0), :]
+                    real = x[comp : comp + 1, :]
+                    imag = x[4 + comp : 5 + comp, :]
                     rows = (field * 4 + comp) * 16
-                    for part, value in enumerate(
-                        (real * cosine - imag * sine, -(real * sine + imag * cosine))
-                    ):
+                    for part, value in enumerate((real * cosine + imag * minus, real * minus - imag * cosine)):
                         high, low = high_low(value)
                         a_ref[parity, part, rows : rows + 16, lanes] = high
                         a_ref[parity, part, 192 + rows : 208 + rows, lanes] = low
@@ -260,7 +262,7 @@
         both = []
         for part in range(2):
             wide = lax.dot_general(
-                a_ref[parity, part], table_buf[parity, part], NT, preferred_element_type=F32
+                a_ref[parity, part, :, 0:slots], table_buf[parity, part, :, 0:slots], NT, preferred_element_type=F32
             )
             fine = wide[0:192, 128:256] + wide[192:384, 128:256]
             both.append(wide[0:192, 0:128] + (wide[192:384, 0:128] + fine))
@@ -288,8 +290,8 @@
         out_shape=jax.ShapeDtypeStruct((8, 48, 256), F32),
         scratch_shapes=[
             pltpu.VMEM((2, 3, slots // 128, 8, 128), F32),
-            pltpu.VMEM((2, 2, 384, slots), BF16),
-            pltpu.VMEM((2, 2, 256, slots), BF16),
+            pltpu.VMEM((2, 2, 384, slots + 128), BF16),
+            pltpu.VMEM((2, 2, 256, slots + 128), BF16),
             pltpu.SemaphoreType.DMA((2,)),
         ],
         compiler_params=pltpu.CompilerParams(vmem_limit_bytes=52 << 20),

time: 60.6 us -> 60.2 us (level)
  no operation moved by 1% of the time
where the time goes in v5:
time: 60.2 us; the launch traced here: 60 us
  blocking collectives  20.8 us (35%)
  starting transfers between devices  14.8 us (25%)
  Pallas kernels  13.5 us (22%)
  waiting for transfers between devices  10.8 us (18%)
    all_to_all x1, blocking collectives, body(): lax.all_to_all(blocks, 'ell', split_axis=0, concat_axis=0, tiled=True)  20.8 us
    all_to_all x1, starting transfers between devices, body(): lax.all_to_all(sums.reshape(64, 3, 4, 128), 'ma', split_axis=0, concat_ax...  14.8 us
    all_to_all x1, waiting for transfers between devices, body(): lax.all_to_all(sums.reshape(64, 3, 4, 128), 'ma', split_axis=0, concat_ax...  10.8 us
    pallas_call x1, Pallas kernels, legendre_sums(): pl.pallas_call(legendre_kernel, in_specs=[pl.BlockSpec(memory_space=pltpu...  4.47 us
    pallas_call x1, Pallas kernels, tables(): pl.pallas_call(tables_kernel, in_specs=[pl.BlockSpec(memory_space=pltpu.S...  4.32 us
    pallas_call x1, Pallas kernels, synthesis(): pl.pallas_call(synthesis_kernel, in_specs=[vmem, vmem, vmem, hbm, vmem],...  3.96 us
  transfers between devices with their start and end apart: 1, of which 1 were waited for; matrix products, arithmetic and copies ran while one was open for 0% of the time, Pallas kernels for 7%

profile of v5, /device:TPU:1, one launch (start us, length us, event | category | flops | bytes accessed | tf_op | source)
XLA Modules:
  0.0 60.0 jit_solution(18363013833235491531)
XLA Ops:
  0.0 0.0 copy-start
  0.0 0.0 copy-start.1
  0.0 4.5 %legendre_sums.1 = f32[768,128]{1,0:T(8,128)} custom-call(s32[2048]{0:T(1024)} %orders_hbm.1, bf16[3,32,32,512]{3,2,1,0:T(8,128)(2,1)} %leg_hbm.1, bf16[32,3,2,4,512]{4,3,2,1,0:T(4,128)(2,1)} %harm_hbm.1), custom_call_target="tpu_custom_call" | custom-call | tf_op jit(solution)/shard_map/legendre_sums/pallas_call | solution.py:106
  4.5 14.8 %all-to-all-start = ((f32[64,3,4,128]{3,2,1,0:T(4,128)}), f32[64,3,4,128]{3,2,1,0:T(4,128)S(1)}, u32[]{:S(2)}, u32[]{:S(2)}) async-start(f32[64,3,4,128]{3,2,1,0:T(4,128)} %bitcast.5), calls=%async_computation | async-start | bytes 786432 | tf_op jit(solution)/shard_map/all_to_all | solution.py:331
  19.3 0.0 copy-done
  19.3 0.0 copy-done.1
  19.4 4.3 %tables.1 = (s32[16,128]{1,0:T(8,128)S(1)}, f32[2,16,16,128]{3,2,1,0:T(8,128)S(1)}, f32[2,16,16,128]{3,2,1,0:T(8,128)S(1)}, bf16[2,2,256,2048]{3,2,1,0:T(8,128)(2,1)}) custom-call(s32[32]{0:T(128)S(1)} %copy-done.1, s32[16,128]{1,0:T(8,128)S(1)} %bitcast.4), custom_call_target="tpu_custom_call" | custom-call | tf_op jit(solution)/shard_map/tables/pallas_call | solution.py:197
  23.7 10.8 %all-to-all-done = f32[64,3,4,128]{3,2,1,0:T(4,128)S(1)} async-done(((f32[64,3,4,128]{3,2,1,0:T(4,128)}), f32[64,3,4,128]{3,2,1,0:T(4,128)S(1)}, u32[]{:S(2)}, u32[]{:S(2)}) %all-to-all-start) | async-done | bytes 393248 | tf_op jit(solution)/shard_map/all_to_all | solution.py:331
  34.5 4.0 %synthesis.1 = f32[8,48,256]{2,1,0:T(8,128)S(1)} custom-call(s32[16,128]{1,0:T(8,128)S(1)} %get-tuple-element.9.lower_ref, f32[2,16,16,128]{3,2,1,0:T(8,128)S(1)} %get-tuple-element.10.cos_ref, f32[2,16,16,128]{3,2,1,0:T(8,128)S(1)} %get-tuple-element.11.sin_ref, bf16[2,2,256,2048]{3,2,1,0:T(8,128)(2,1)} %get-tuple-element.12.table_ref, f32[768,128]{1,0:T(8,128)S(1)} %bitcast.3), custom_call_target="tpu_custom_call" | custom-call | tf_op jit(solution)/shard_map/synthesis/pallas_call | solution.py:286
  38.5 20.8 %all_to_all.10.parts_ref = f32[8,48,256]{2,1,0:T(8,128)S(1)} all-to-all(f32[8,48,256]{2,1,0:T(8,128)S(1)} %synthesis.1), channel_id=1, replica_groups=mesh['ma'=64,'ell'=8] {'ell'}, dimensions={0} | all-to-all | bytes 786432 | tf_op jit(solution)/shard_map/all_to_all | solution.py:334
  59.3 0.7 %total.1 = f32[1,3,4,1024]{3,2,1,0:T(4,128)} custom-call(f32[8,48,256]{2,1,0:T(8,128)S(1)} %all_to_all.10.parts_ref), custom_call_target="tpu_custom_call" | custom-call | tf_op jit(solution)/shard_map/total/pallas_call | solution.py:318
Async XLA Ops:
  0.0 19.3 %copy-start = (s32[2048]{0:T(1024)S(1)}, s32[2048]{0:T(1024)}, u32[]{:S(2)}) copy-start(s32[2048]{0:T(1024)} %orders_hbm.1) | copy-start | bytes 24580
  0.0 19.3 %copy-start.1 = (s32[32]{0:T(128)S(1)}, s32[32]{0:T(128)}, u32[]{:S(2)}) copy-start(s32[32]{0:T(128)} %cycle_ref.1) | copy-start | bytes 388
  4.5 30.0 %all-to-all-start = ((f32[64,3,4,128]{3,2,1,0:T(4,128)}), f32[64,3,4,128]{3,2,1,0:T(4,128)S(1)}, u32[]{:S(2)}, u32[]{:S(2)}) async-start(f32[64,3,4,128]{3,2,1,0:T(4,128)} %bitcast.5), calls=%async_computation | async-start | bytes 786432 | tf_op jit(solution)/shard_map/all_to_all | solution.py:331

commit v6 on v5

--- a/solution.py
+++ b/solution.py
@@ -97,7 +97,7 @@
             acc_ref[side * 3 + 2, :, lanes] = both[:, 32 * side + 16 : 32 * side + 32]
     for side in range(2):
         for field in range(3):
-            start = side * pairs * 12 + field * 4 + group
+            start = (1 - side) * pairs * 12 + field * 4 + group
             out_ref[pl.ds(start, pairs, stride=12), :] = acc_ref[side * 3 + field]
 
 
@@ -145,7 +145,7 @@
     tiles = slots // 128
     shift = cycle_ref[lax.axis_index("ma") % cycle_ref.shape[0]] % 2
     row = lax.broadcasted_iota(jnp.int32, (16, 128), 0)
-    turned = slots_ref[...].astype(F32).T
+    turned = jnp.concatenate([slots_ref[8:16, :], slots_ref[0:8, :]], axis=0).astype(F32).T
     pieces = []
     for middle in range(2):
         for device in range(4):
@@ -328,7 +328,10 @@
 
 def body(legendre, harmonics, slot_orders, cycle_index):
     sums = legendre_sums(legendre, harmonics, slot_orders)
-    moved = lax.all_to_all(sums.reshape(64, 3, 4, 128), "ma", split_axis=0, concat_axis=0, tiled=True)
+    swapped = [[device ^ 32 for device in range(64)]]
+    moved = lax.all_to_all(
+        sums.reshape(64, 3, 4, 128), "ma", split_axis=0, concat_axis=0, axis_index_groups=swapped, tiled=True
+    )
     lower, cosine, sine, table = tables(cycle_index, slot_orders)
     blocks = synthesis(lower, cosine, sine, table, moved.reshape(768, 128))
     arrived = lax.all_to_all(blocks, "ell", split_axis=0, concat_axis=0, tiled=True)

time: 60.2 us -> 58.8 us (0.977)
  waiting for transfers between devices: 10.8 us -> 6.93 us
  starting transfers between devices: 14.8 us -> 17.8 us
  blocking collectives: 20.8 us -> 20 us
    all_to_all x1, waiting for transfers between devices: 10.8 us -> 6.93 us  [body(): lax.all_to_all(sums.reshape(64, 3, 4, 128), 'ma', split_axis=0, concat_ax...]
    all_to_all x1, starting transfers between devices: 14.8 us -> 17.8 us  [body(): lax.all_to_all(sums.reshape(64, 3, 4, 128), 'ma', split_axis=0, concat_ax...]
    all_to_all x1, blocking collectives: 20.8 us -> 20 us  [body(): lax.all_to_all(blocks, 'ell', split_axis=0, concat_axis=0, tiled=True)]
where the time goes in v6:
time: 58.8 us; the launch traced here: 58.3 us
  blocking collectives  20 us (34%)
  starting transfers between devices  17.8 us (30%)
  Pallas kernels  13.5 us (23%)
  waiting for transfers between devices  6.93 us (12%)
    all_to_all x1, blocking collectives, body(): lax.all_to_all(blocks, 'ell', split_axis=0, concat_axis=0, tiled=True)  20 us
    all_to_all x1, starting transfers between devices, body(): lax.all_to_all(sums.reshape(64, 3, 4, 128), 'ma', split_axis=0, concat_ax...  17.8 us
    all_to_all x1, waiting for transfers between devices, body(): lax.all_to_all(sums.reshape(64, 3, 4, 128), 'ma', split_axis=0, concat_ax...  6.93 us
    pallas_call x1, Pallas kernels, legendre_sums(): pl.pallas_call(legendre_kernel, in_specs=[pl.BlockSpec(memory_space=pltpu...  4.47 us
    pallas_call x1, Pallas kernels, tables(): pl.pallas_call(tables_kernel, in_specs=[pl.BlockSpec(memory_space=pltpu.S...  4.32 us
    pallas_call x1, Pallas kernels, synthesis(): pl.pallas_call(synthesis_kernel, in_specs=[vmem, vmem, vmem, hbm, vmem],...  3.96 us
  transfers between devices with their start and end apart: 1, of which 1 were waited for; matrix products, arithmetic and copies ran while one was open for 0% of the time, Pallas kernels for 7%

profile of v6, /device:TPU:1, one launch (start us, length us, event | category | flops | bytes accessed | tf_op | source)
XLA Modules:
  0.0 58.3 jit_solution(9066248111921061002)
XLA Ops:
  0.0 0.0 copy-start
  0.0 0.0 copy-start.1
  0.0 4.5 %legendre_sums.1 = f32[768,128]{1,0:T(8,128)} custom-call(s32[2048]{0:T(1024)} %orders_hbm.1, bf16[3,32,32,512]{3,2,1,0:T(8,128)(2,1)} %leg_hbm.1, bf16[32,3,2,4,512]{4,3,2,1,0:T(4,128)(2,1)} %harm_hbm.1), custom_call_target="tpu_custom_call" | custom-call | tf_op jit(solution)/shard_map/legendre_sums/pallas_call | solution.py:106
  4.5 17.8 %all-to-all-start = ((f32[64,3,4,128]{3,2,1,0:T(4,128)}), f32[64,3,4,128]{3,2,1,0:T(4,128)S(1)}, u32[]{:S(2)}, u32[]{:S(2)}) async-start(f32[64,3,4,128]{3,2,1,0:T(4,128)} %bitcast.5), calls=%async_computation | async-start | bytes 786432 | tf_op jit(solution)/shard_map/all_to_all | solution.py:332
  22.3 0.0 copy-done
  22.3 0.0 copy-done.1
  22.3 4.3 %tables.1 = (s32[16,128]{1,0:T(8,128)S(1)}, f32[2,16,16,128]{3,2,1,0:T(8,128)S(1)}, f32[2,16,16,128]{3,2,1,0:T(8,128)S(1)}, bf16[2,2,256,2048]{3,2,1,0:T(8,128)(2,1)}) custom-call(s32[32]{0:T(128)S(1)} %copy-done.1, s32[16,128]{1,0:T(8,128)S(1)} %bitcast.4), custom_call_target="tpu_custom_call" | custom-call | tf_op jit(solution)/shard_map/tables/pallas_call | solution.py:197
  26.7 6.9 %all-to-all-done = f32[64,3,4,128]{3,2,1,0:T(4,128)S(1)} async-done(((f32[64,3,4,128]{3,2,1,0:T(4,128)}), f32[64,3,4,128]{3,2,1,0:T(4,128)S(1)}, u32[]{:S(2)}, u32[]{:S(2)}) %all-to-all-start) | async-done | bytes 393248 | tf_op jit(solution)/shard_map/all_to_all | solution.py:332
  33.6 4.0 %synthesis.1 = f32[8,48,256]{2,1,0:T(8,128)S(1)} custom-call(s32[16,128]{1,0:T(8,128)S(1)} %get-tuple-element.9.lower_ref, f32[2,16,16,128]{3,2,1,0:T(8,128)S(1)} %get-tuple-element.10.cos_ref, f32[2,16,16,128]{3,2,1,0:T(8,128)S(1)} %get-tuple-element.11.sin_ref, bf16[2,2,256,2048]{3,2,1,0:T(8,128)(2,1)} %get-tuple-element.12.table_ref, f32[768,128]{1,0:T(8,128)S(1)} %bitcast.3), custom_call_target="tpu_custom_call" | custom-call | tf_op jit(solution)/shard_map/synthesis/pallas_call | solution.py:286
  37.6 20.0 %all_to_all.10.parts_ref = f32[8,48,256]{2,1,0:T(8,128)S(1)} all-to-all(f32[8,48,256]{2,1,0:T(8,128)S(1)} %synthesis.1), channel_id=1, replica_groups=mesh['ma'=64,'ell'=8] {'ell'}, dimensions={0} | all-to-all | bytes 786432 | tf_op jit(solution)/shard_map/all_to_all | solution.py:337
  57.6 0.7 %total.1 = f32[1,3,4,1024]{3,2,1,0:T(4,128)} custom-call(f32[8,48,256]{2,1,0:T(8,128)S(1)} %all_to_all.10.parts_ref), custom_call_target="tpu_custom_call" | custom-call | tf_op jit(solution)/shard_map/total/pallas_call | solution.py:318
Async XLA Ops:
  0.0 22.3 %copy-start = (s32[2048]{0:T(1024)S(1)}, s32[2048]{0:T(1024)}, u32[]{:S(2)}) copy-start(s32[2048]{0:T(1024)} %orders_hbm.1) | copy-start | bytes 24580
  0.0 22.3 %copy-start.1 = (s32[32]{0:T(128)S(1)}, s32[32]{0:T(128)}, u32[]{:S(2)}) copy-start(s32[32]{0:T(128)} %cycle_ref.1) | copy-start | bytes 388
  4.5 29.1 %all-to-all-start = ((f32[64,3,4,128]{3,2,1,0:T(4,128)}), f32[64,3,4,128]{3,2,1,0:T(4,128)S(1)}, u32[]{:S(2)}, u32[]{:S(2)}) async-start(f32[64,3,4,128]{3,2,1,0:T(4,128)} %bitcast.5), calls=%async_computation | async-start | bytes 786432 | tf_op jit(solution)/shard_map/all_to_all | solution.py:332

commit v7 on v6

--- a/solution.py
+++ b/solution.py
@@ -275,8 +275,8 @@
             for row in range(12):
                 place = slice(row * 4, row * 4 + 4)
                 source = slice(row * 16 + block * 4, row * 16 + block * 4 + 4)
-                out_ref[block, place, lanes] = near[source, :]
-                out_ref[block + 4, place, lanes] = far[source, :]
+                out_ref[block + 4, place, lanes] = near[source, :]
+                out_ref[block, place, lanes] = far[source, :]
 
 
 def synthesis(lower, cosine, sine, table, sums):
@@ -334,7 +334,10 @@
     )
     lower, cosine, sine, table = tables(cycle_index, slot_orders)
     blocks = synthesis(lower, cosine, sine, table, moved.reshape(768, 128))
-    arrived = lax.all_to_all(blocks, "ell", split_axis=0, concat_axis=0, tiled=True)
+    swapped = [[device ^ 4 for device in range(8)]]
+    arrived = lax.all_to_all(
+        blocks, "ell", split_axis=0, concat_axis=0, axis_index_groups=swapped, tiled=True
+    )
     return total(arrived)
 
 

time: 58.8 us -> 55.3 us (0.940)
  blocking collectives: 20 us -> 16.9 us
    all_to_all x1, blocking collectives: 20 us -> 16.9 us  [body(): lax.all_to_all(blocks, 'ell', split_axis=0, concat_axis=0, axis_index_gro...]
  transfers between devices with their start and end apart: 1 -> 1, of which waited for: 1 -> 1; matrix products, arithmetic and copies ran while one was open for 0% -> 0% of each run, Pallas kernels for 7% -> 8%
where the time goes in v7:
time: 55.3 us; the launch traced here: 55.1 us
  starting transfers between devices  17.8 us (32%)
  blocking collectives  16.9 us (31%)
  Pallas kernels  13.5 us (24%)
  waiting for transfers between devices  6.93 us (13%)
    all_to_all x1, starting transfers between devices, body(): lax.all_to_all(sums.reshape(64, 3, 4, 128), 'ma', split_axis=0, concat_ax...  17.8 us
    all_to_all x1, blocking collectives, body(): lax.all_to_all(blocks, 'ell', split_axis=0, concat_axis=0, axis_index_gro...  16.9 us
    all_to_all x1, waiting for transfers between devices, body(): lax.all_to_all(sums.reshape(64, 3, 4, 128), 'ma', split_axis=0, concat_ax...  6.93 us
    pallas_call x1, Pallas kernels, legendre_sums(): pl.pallas_call(legendre_kernel, in_specs=[pl.BlockSpec(memory_space=pltpu...  4.47 us
    pallas_call x1, Pallas kernels, tables(): pl.pallas_call(tables_kernel, in_specs=[pl.BlockSpec(memory_space=pltpu.S...  4.32 us
    pallas_call x1, Pallas kernels, synthesis(): pl.pallas_call(synthesis_kernel, in_specs=[vmem, vmem, vmem, hbm, vmem],...  3.96 us
  transfers between devices with their start and end apart: 1, of which 1 were waited for; matrix products, arithmetic and copies ran while one was open for 0% of the time, Pallas kernels for 8%

profile of v7, /device:TPU:1, one launch (start us, length us, event | category | flops | bytes accessed | tf_op | source)
XLA Modules:
  0.0 55.1 jit_solution(3795176544651186988)
XLA Ops:
  0.0 0.0 copy-start
  0.0 0.0 copy-start.1
  0.0 4.5 %legendre_sums.1 = f32[768,128]{1,0:T(8,128)} custom-call(s32[2048]{0:T(1024)} %orders_hbm.1, bf16[3,32,32,512]{3,2,1,0:T(8,128)(2,1)} %leg_hbm.1, bf16[32,3,2,4,512]{4,3,2,1,0:T(4,128)(2,1)} %harm_hbm.1), custom_call_target="tpu_custom_call" | custom-call | tf_op jit(solution)/shard_map/legendre_sums/pallas_call | solution.py:106
  4.5 17.8 %all-to-all-start = ((f32[64,3,4,128]{3,2,1,0:T(4,128)}), f32[64,3,4,128]{3,2,1,0:T(4,128)S(1)}, u32[]{:S(2)}, u32[]{:S(2)}) async-start(f32[64,3,4,128]{3,2,1,0:T(4,128)} %bitcast.5), calls=%async_computation | async-start | bytes 786432 | tf_op jit(solution)/shard_map/all_to_all | solution.py:332
  22.3 0.0 copy-done
  22.3 0.0 copy-done.1
  22.3 4.3 %tables.1 = (s32[16,128]{1,0:T(8,128)S(1)}, f32[2,16,16,128]{3,2,1,0:T(8,128)S(1)}, f32[2,16,16,128]{3,2,1,0:T(8,128)S(1)}, bf16[2,2,256,2048]{3,2,1,0:T(8,128)(2,1)}) custom-call(s32[32]{0:T(128)S(1)} %copy-done.1, s32[16,128]{1,0:T(8,128)S(1)} %bitcast.4), custom_call_target="tpu_custom_call" | custom-call | tf_op jit(solution)/shard_map/tables/pallas_call | solution.py:197
  26.7 6.9 %all-to-all-done = f32[64,3,4,128]{3,2,1,0:T(4,128)S(1)} async-done(((f32[64,3,4,128]{3,2,1,0:T(4,128)}), f32[64,3,4,128]{3,2,1,0:T(4,128)S(1)}, u32[]{:S(2)}, u32[]{:S(2)}) %all-to-all-start) | async-done | bytes 393248 | tf_op jit(solution)/shard_map/all_to_all | solution.py:332
  33.6 4.0 %synthesis.1 = f32[8,48,256]{2,1,0:T(8,128)S(1)} custom-call(s32[16,128]{1,0:T(8,128)S(1)} %get-tuple-element.9.lower_ref, f32[2,16,16,128]{3,2,1,0:T(8,128)S(1)} %get-tuple-element.10.cos_ref, f32[2,16,16,128]{3,2,1,0:T(8,128)S(1)} %get-tuple-element.11.sin_ref, bf16[2,2,256,2048]{3,2,1,0:T(8,128)(2,1)} %get-tuple-element.12.table_ref, f32[768,128]{1,0:T(8,128)S(1)} %bitcast.3), custom_call_target="tpu_custom_call" | custom-call | tf_op jit(solution)/shard_map/synthesis/pallas_call | solution.py:286
  37.6 16.9 %all_to_all.10.parts_ref = f32[8,48,256]{2,1,0:T(8,128)S(1)} all-to-all(f32[8,48,256]{2,1,0:T(8,128)S(1)} %synthesis.1), channel_id=1, replica_groups={{4,5,6,7,0,1,2,3},{12,13,14,15,8,9,10,11},{20,21,22,23,16,17,18,19},{28..., dimensions={0} | all-to-all | bytes 786432 | tf_op jit(solution)/shard_map/all_to_all | solution.py:338
  54.4 0.7 %total.1 = f32[1,3,4,1024]{3,2,1,0:T(4,128)} custom-call(f32[8,48,256]{2,1,0:T(8,128)S(1)} %all_to_all.10.parts_ref), custom_call_target="tpu_custom_call" | custom-call | tf_op jit(solution)/shard_map/total/pallas_call | solution.py:318
Async XLA Ops:
  0.0 22.3 %copy-start = (s32[2048]{0:T(1024)S(1)}, s32[2048]{0:T(1024)}, u32[]{:S(2)}) copy-start(s32[2048]{0:T(1024)} %orders_hbm.1) | copy-start | bytes 24580
  0.0 22.3 %copy-start.1 = (s32[32]{0:T(128)S(1)}, s32[32]{0:T(128)}, u32[]{:S(2)}) copy-start(s32[32]{0:T(128)} %cycle_ref.1) | copy-start | bytes 388
  4.5 29.1 %all-to-all-start = ((f32[64,3,4,128]{3,2,1,0:T(4,128)}), f32[64,3,4,128]{3,2,1,0:T(4,128)S(1)}, u32[]{:S(2)}, u32[]{:S(2)}) async-start(f32[64,3,4,128]{3,2,1,0:T(4,128)} %bitcast.5), calls=%async_computation | async-start | bytes 786432 | tf_op jit(solution)/shard_map/all_to_all | solution.py:332

commit v8 on v7

--- a/solution.py
+++ b/solution.py
@@ -275,8 +275,8 @@
             for row in range(12):
                 place = slice(row * 4, row * 4 + 4)
                 source = slice(row * 16 + block * 4, row * 16 + block * 4 + 4)
-                out_ref[block + 4, place, lanes] = near[source, :]
-                out_ref[block, place, lanes] = far[source, :]
+                out_ref[4 - block, place, lanes] = near[source, :]
+                out_ref[-block % 8, place, lanes] = far[source, :]
 
 
 def synthesis(lower, cosine, sine, table, sums):
@@ -334,7 +334,7 @@
     )
     lower, cosine, sine, table = tables(cycle_index, slot_orders)
     blocks = synthesis(lower, cosine, sine, table, moved.reshape(768, 128))
-    swapped = [[device ^ 4 for device in range(8)]]
+    swapped = [[(4 - rank) % 8 for rank in range(8)]]
     arrived = lax.all_to_all(
         blocks, "ell", split_axis=0, concat_axis=0, axis_index_groups=swapped, tiled=True
     )

time: 55.3 us -> 55.7 us (level)
  no operation moved by 1% of the time
where the time goes in v8:
time: 55.7 us; the launch traced here: 55.5 us
  starting transfers between devices  17.8 us (32%)
  blocking collectives  17.3 us (31%)
  Pallas kernels  13.5 us (24%)
  waiting for transfers between devices  6.93 us (12%)
    all_to_all x1, starting transfers between devices, body(): lax.all_to_all(sums.reshape(64, 3, 4, 128), 'ma', split_axis=0, concat_ax...  17.8 us
    all_to_all x1, blocking collectives, body(): lax.all_to_all(blocks, 'ell', split_axis=0, concat_axis=0, axis_index_gro...  17.3 us
    all_to_all x1, waiting for transfers between devices, body(): lax.all_to_all(sums.reshape(64, 3, 4, 128), 'ma', split_axis=0, concat_ax...  6.93 us
    pallas_call x1, Pallas kernels, legendre_sums(): pl.pallas_call(legendre_kernel, in_specs=[pl.BlockSpec(memory_space=pltpu...  4.47 us
    pallas_call x1, Pallas kernels, tables(): pl.pallas_call(tables_kernel, in_specs=[pl.BlockSpec(memory_space=pltpu.S...  4.32 us
    pallas_call x1, Pallas kernels, synthesis(): pl.pallas_call(synthesis_kernel, in_specs=[vmem, vmem, vmem, hbm, vmem],...  3.96 us
  transfers between devices with their start and end apart: 1, of which 1 were waited for; matrix products, arithmetic and copies ran while one was open for 0% of the time, Pallas kernels for 8%

profile of v8, /device:TPU:1, one launch (start us, length us, event | category | flops | bytes accessed | tf_op | source)
XLA Modules:
  0.0 55.5 jit_solution(16369444024093870535)
XLA Ops:
  0.0 0.0 copy-start
  0.0 0.0 copy-start.1
  0.0 4.5 %legendre_sums.1 = f32[768,128]{1,0:T(8,128)} custom-call(s32[2048]{0:T(1024)} %orders_hbm.1, bf16[3,32,32,512]{3,2,1,0:T(8,128)(2,1)} %leg_hbm.1, bf16[32,3,2,4,512]{4,3,2,1,0:T(4,128)(2,1)} %harm_hbm.1), custom_call_target="tpu_custom_call" | custom-call | tf_op jit(solution)/shard_map/legendre_sums/pallas_call | solution.py:106
  4.5 17.8 %all-to-all-start = ((f32[64,3,4,128]{3,2,1,0:T(4,128)}), f32[64,3,4,128]{3,2,1,0:T(4,128)S(1)}, u32[]{:S(2)}, u32[]{:S(2)}) async-start(f32[64,3,4,128]{3,2,1,0:T(4,128)} %bitcast.5), calls=%async_computation | async-start | bytes 786432 | tf_op jit(solution)/shard_map/all_to_all | solution.py:332
  22.3 0.0 copy-done
  22.3 0.0 copy-done.1
  22.3 4.3 %tables.1 = (s32[16,128]{1,0:T(8,128)S(1)}, f32[2,16,16,128]{3,2,1,0:T(8,128)S(1)}, f32[2,16,16,128]{3,2,1,0:T(8,128)S(1)}, bf16[2,2,256,2048]{3,2,1,0:T(8,128)(2,1)}) custom-call(s32[32]{0:T(128)S(1)} %copy-done.1, s32[16,128]{1,0:T(8,128)S(1)} %bitcast.4), custom_call_target="tpu_custom_call" | custom-call | tf_op jit(solution)/shard_map/tables/pallas_call | solution.py:197
  26.7 6.9 %all-to-all-done = f32[64,3,4,128]{3,2,1,0:T(4,128)S(1)} async-done(((f32[64,3,4,128]{3,2,1,0:T(4,128)}), f32[64,3,4,128]{3,2,1,0:T(4,128)S(1)}, u32[]{:S(2)}, u32[]{:S(2)}) %all-to-all-start) | async-done | bytes 393248 | tf_op jit(solution)/shard_map/all_to_all | solution.py:332
  33.6 4.0 %synthesis.1 = f32[8,48,256]{2,1,0:T(8,128)S(1)} custom-call(s32[16,128]{1,0:T(8,128)S(1)} %get-tuple-element.9.lower_ref, f32[2,16,16,128]{3,2,1,0:T(8,128)S(1)} %get-tuple-element.10.cos_ref, f32[2,16,16,128]{3,2,1,0:T(8,128)S(1)} %get-tuple-element.11.sin_ref, bf16[2,2,256,2048]{3,2,1,0:T(8,128)(2,1)} %get-tuple-element.12.table_ref, f32[768,128]{1,0:T(8,128)S(1)} %bitcast.3), custom_call_target="tpu_custom_call" | custom-call | tf_op jit(solution)/shard_map/synthesis/pallas_call | solution.py:286
  37.6 17.3 %all_to_all.10.parts_ref = f32[8,48,256]{2,1,0:T(8,128)S(1)} all-to-all(f32[8,48,256]{2,1,0:T(8,128)S(1)} %synthesis.1), channel_id=1, replica_groups={{4,3,2,1,0,7,6,5},{12,11,10,9,8,15,14,13},{20,19,18,17,16,23,22,21},{28..., dimensions={0} | all-to-all | bytes 786432 | tf_op jit(solution)/shard_map/all_to_all | solution.py:338
  54.8 0.7 %total.1 = f32[1,3,4,1024]{3,2,1,0:T(4,128)} custom-call(f32[8,48,256]{2,1,0:T(8,128)S(1)} %all_to_all.10.parts_ref), custom_call_target="tpu_custom_call" | custom-call | tf_op jit(solution)/shard_map/total/pallas_call | solution.py:318
Async XLA Ops:
  0.0 22.3 %copy-start = (s32[2048]{0:T(1024)S(1)}, s32[2048]{0:T(1024)}, u32[]{:S(2)}) copy-start(s32[2048]{0:T(1024)} %orders_hbm.1) | copy-start | bytes 24580
  0.0 22.3 %copy-start.1 = (s32[32]{0:T(128)S(1)}, s32[32]{0:T(128)}, u32[]{:S(2)}) copy-start(s32[32]{0:T(128)} %cycle_ref.1) | copy-start | bytes 388
  4.5 29.1 %all-to-all-start = ((f32[64,3,4,128]{3,2,1,0:T(4,128)}), f32[64,3,4,128]{3,2,1,0:T(4,128)S(1)}, u32[]{:S(2)}, u32[]{:S(2)}) async-start(f32[64,3,4,128]{3,2,1,0:T(4,128)} %bitcast.5), calls=%async_computation | async-start | bytes 786432 | tf_op jit(solution)/shard_map/all_to_all | solution.py:332
